TPU v7x, 32 devices: a whole 2x2x4 slice. The times are simulated.
32 devices in a mesh: member: 2 (over y), blk: 16 (over z, x, core).
Axes of the slice: x: 2, y: 2, z: 4, core: 2. Of those that a mesh axis runs over, the one named last changes fastest.
Arguments:
- heat_anomaly: float32 [8, 1536, 512], P('member', 'blk'), parts along dimension 0, may hold values from -6 to 6
- saltiness_anomaly: float32 [8, 1536, 512], P('member', 'blk'), parts along dimension 0, may hold values from -6 to 6
- first_axis_flow: float32 [8, 1536, 512], P('member', 'blk'), parts along dimension 0, may hold values from -4 to 4
- second_axis_flow: float32 [8, 1536, 512], P('member', 'blk'), parts along dimension 0, may hold values from -4 to 4
- layer_spacing: float32 [4], replicated, may hold values from 0.5 to 4
- diagonal_shift: float32 [1536, 512], P('blk'), may hold values from 0.02 to 0.2
- water_tile_flags: int32 [16, 8], P('blk'), may hold values 0 or 1
Outputs:
- new_temperature: bfloat16 [8, 1536, 512], P('member', 'blk'), parts along dimension 0
- new_salinity: bfloat16 [8, 1536, 512], P('member', 'blk'), parts along dimension 0
- new_u: bfloat16 [8, 1536, 512], P('member', 'blk'), parts along dimension 0
- new_v: bfloat16 [8, 1536, 512], P('member', 'blk'), parts along dimension 0
- height: float32 [3072, 512], P(('member', 'blk')), parts along dimension 0
- residual: float32 [3072, 512], P(('member', 'blk')), parts along dimension 0
There are 2 independent parts, one for each index of `member`. A program takes and returns all parts, laid end to end along the dimension named above; an argument that names none is the same for every part. Nothing has to cross between parts.
Inputs may be any that keep to these rules, and one draw needn't show every extreme that they name: `water_tile_flags`: 1 marks an ocean block, 0 a land block.
All inputs are finite; a program needn't handle non-finite values.
Results may differ from a plain program's by a relative error of at most 0.001.
Values sent between devices are 32-bit elements; how exact they have to be, the bound alone decides.
A program may use at most 128 MiB of HBM per device.

v0:
```python
import functools

import jax
import jax.numpy as jnp
import numpy as np
from jax import lax
from jax.experimental import pallas as pl
from jax.experimental.pallas import tpu as pltpu
from jax.sharding import PartitionSpec as P

SSTEP = 4
CG_BLOCKS = 3
SWEEPS = SSTEP * CG_BLOCKS
FIELDS = SWEEPS + 1
MOMENTS = 2 * SWEEPS + 1
COURANT = 0.2
SHIFT = SWEEPS + 2
WEST = -(-(2 * SWEEPS + 2) // 8) * 8
EAST = -(-(SWEEPS + 2) // 8) * 8
F32 = jnp.float32
BF16 = jnp.bfloat16


def shift_table(extent):
    table = np.zeros((extent, extent), np.float32)
    for source in range(extent - 1):
        if source == 0:
            table[1, 0] = table[0, 0] = 0.5
        else:
            table[source + 1, source] = 0.25
            table[source, source] = 0.5
            table[source - 1, source] = 0.25
    return table


def tree(terms):
    while len(terms) > 1:
        terms = [
            terms[i] + terms[i + 1] if i + 1 < len(terms) else terms[i]
            for i in range(0, len(terms), 2)
        ]
    return terms[0]


def quadratic(gram, left, right):
    rows = []
    for i, li in enumerate(left):
        if li is not None:
            rows.append(li * tree([gram[i][j] * rj for j, rj in enumerate(right) if rj is not None]))
    return tree(rows)


def plus(a, b):
    if a is None:
        return b
    if b is None:
        return a
    return a + b


def scaled(scale, a):
    return None if a is None else scale * a


def inner_steps(gram, sweeps):
    extent = sweeps + 1
    table = shift_table(extent)
    one = jnp.ones_like(gram[0][0])
    along = [one] + [None] * sweeps
    resid = [one] + [None] * sweeps
    offset = [None] * extent
    norm_now = quadratic(gram, resid, resid)
    for sweep in range(sweeps):
        image = []
        for i in range(extent):
            total = None
            for j in range(extent):
                if table[i, j] != 0.0:
                    total = plus(total, scaled(float(table[i, j]), along[j]))
            image.append(total)
        alpha = norm_now / quadratic(gram, along, image)
        offset = [plus(o, scaled(alpha, a)) for o, a in zip(offset, along)]
        resid = [plus(r, scaled(-alpha, a)) for r, a in zip(resid, image)]
        if sweep + 1 < sweeps:
            norm_next = quadratic(gram, resid, resid)
            beta = norm_next / norm_now
            along = [plus(r, scaled(beta, a)) for r, a in zip(resid, along)]
            norm_now = norm_next
    return offset, resid


def kernel(
    n,
    heat, salt, uvel, vvel, spacing, damp, flags,
    bh, bs, bu, bv, basis, mom,
    ue, ve, he, se, ef, nf, de, tu, tv, acc, edges,
    uv_tx, hs_tx, uv_rx, hs_rx, aw_tx, ae_tx, a4, fw_tx, fe_tx, fw_rx, fe_rx, slots,
    space, marks,
    lsem, ssem, rsem, gs_sem, gr_sem,
):
    levels, rows, lanes = ue.shape
    me = lax.axis_index("blk")
    right, left = lax.rem(me + 1, n), lax.rem(me + n - 1, n)
    late = rows - WEST
    split = late - 8

    def part(ref, buf, lo, hi, sem):
        return pltpu.make_async_copy(
            ref.at[:, pl.ds(lo, hi - lo)], buf.at[:, pl.ds(lo, hi - lo)], lsem.at[sem]
        )

    loads = [
        pltpu.make_async_copy(flags, marks, lsem.at[0]),
        pltpu.make_async_copy(spacing, space, lsem.at[1]),
        part(uvel, ue, split, rows, 2),
        part(vvel, ve, split, rows, 3),
        pltpu.make_async_copy(damp, de, lsem.at[4]),
        part(uvel, ue, 0, split, 5),
        part(vvel, ve, 0, split, 6),
        pltpu.make_async_copy(heat, he, lsem.at[7]),
        pltpu.make_async_copy(salt, se, lsem.at[8]),
    ]
    for load in loads:
        load.start()

    barrier = pltpu.get_barrier_semaphore()
    for k in range(1, n):
        pl.semaphore_signal(
            barrier, inc=1, device_id={"blk": lax.rem(me + k, n)},
            device_id_type=pl.DeviceIdType.MESH,
        )

    lane = lax.broadcasted_iota(jnp.int32, (8, lanes), 1)
    sub = lax.broadcasted_iota(jnp.int32, (8, lanes), 0)
    top, bottom = sub == 0, sub == 7
    zero = jnp.zeros((8, lanes), F32)

    def north_of(x):
        return pltpu.roll(x, lanes - 1, 1)

    def south_of(x):
        return pltpu.roll(x, 1, 1)

    def sides(x):
        return jnp.where(lane == lanes - 1, 0.0, north_of(x)), jnp.where(lane == 0, 0.0, south_of(x))

    def up_one(x):
        return pltpu.roll(x, 7, 0)

    def down_one(x):
        return pltpu.roll(x, 1, 0)

    loads[0].wait()
    loads[1].wait()
    tiles = marks.shape[1]
    lane_tile = lane // (lanes // tiles)
    own = zero
    for k in range(tiles):
        own = jnp.where(lane_tile == k, marks[0, k].astype(F32), own)
    ahead = jnp.where(lane == lanes - 1, 0.0, own * north_of(own))
    whole_w = jnp.zeros((8, 128), F32)
    for j in range(levels):
        whole_w = whole_w + space[j]
    portions = [jnp.full((8, 128), space[j], F32) / whole_w for j in range(levels)]

    def wide(x):
        return jnp.concatenate([x] * (lanes // 128), axis=1)

    weight = [wide(x) for x in portions]
    level_weight = zero
    for j in range(levels):
        level_weight = jnp.where(sub % levels == j, weight[j], level_weight)

    def gather_row(refs, row):
        block, place = row // 8 * 8, row % 8
        packed = None
        for i, ref in enumerate(refs):
            for level in range(levels):
                x = ref[level, pl.ds(block, 8)]
                spot = i * levels + level
                if (spot - place) % 8:
                    x = pltpu.roll(x, (spot - place) % 8, 0)
                packed = x if packed is None else jnp.where(sub == spot, x, packed)
        return packed

    def pick(packed, block, spot, place):
        return jnp.where(sub == spot, pltpu.roll(block, (spot - place) % 8, 0) if (spot - place) % 8 else block, packed)

    def advect(q, fe, fw, fn):
        return own * (q - (0.5 * COURANT) * ((fe - fw) + (fn - south_of(fn))))

    def flows(first, last, fresh, fields, outs, slot, keep):
        u_like = fields[0]
        ends = [zero, zero]
        for level in range(levels):
            def east_of(r):
                if keep:
                    u0 = u_like[level, pl.ds(r, 8)]
                    if r + 8 < rows:
                        return u0 + jnp.where(bottom, up_one(u_like[level, pl.ds(r + 8, 8)]), up_one(u0))
                    return jnp.where(bottom, 0.0, u0 + up_one(u0))
                return ef[level, pl.ds(r, 8)]

            def flux(ref, r, east):
                q0 = ref[level, pl.ds(r, 8)]
                qp = up_one(q0)
                if r + 8 < rows:
                    qp = jnp.where(bottom, up_one(ref[level, pl.ds(r + 8, 8)]), qp)
                return q0, east * jnp.where(east > 0.0, q0, qp)

            if first == 0:
                before = [zero, zero]
            else:
                e = east_of(first - 8)
                before = [down_one(flux(ref, first - 8, e)[1]) for ref in fields]
            pending = None
            for r in range(first, last, 8):
                here = pl.ds(r, 8)
                east = east_of(r)
                if keep:
                    v0 = fields[1][level, here]
                    north = (v0 + north_of(v0)) * ahead
                    ef[level, here] = east
                    nf[level, here] = north
                else:
                    north = nf[level, here]
                news = []
                for i, ref in enumerate(fields):
                    q0, fe = flux(ref, r, east)
                    shifted = down_one(fe)
                    fw = jnp.where(top, before[i], shifted)
                    before[i] = shifted
                    fn = north * jnp.where(north > 0.0, q0, north_of(q0))
                    new = advect(q0, fe, fw, fn)
                    news.append(new)
                    if keep:
                        total = (tu, tv)[i]
                        term = weight[level] * new
                        total[here] = term if level == 0 else total[here] + term
                    spot = i * levels + level
                    if r == 0:
                        ends[0] = pick(ends[0], new, spot, 0)
                    if r + 8 == rows:
                        ends[1] = pick(ends[1], new, spot, 7)
                if pending is None:
                    pending = news
                else:
                    for i, out in enumerate(outs):
                        out[level, pl.ds(r - 8, 16)] = jnp.concatenate([pending[i], news[i]], axis=0).astype(BF16)
                    pending = None
        if first == 0:
            edges[slot] = ends[0]
        if last == rows:
            edges[slot + 1] = ends[1]

    def forcing(r, low, high):
        t0, x0 = tv[pl.ds(r, 8)], tu[pl.ds(r, 8)]
        north, south = sides(t0)
        after = jnp.where(bottom, up_one(tu[pl.ds(r + 8, 8)]) if r + 8 < high else 0.0, up_one(x0))
        prior = jnp.where(top, down_one(tu[pl.ds(r - 8, 8)]) if r > low else 0.0, down_one(x0))
        return (0.5 * own) * ((after - prior) + (north - south))

    for k in (2, 3):
        loads[k].wait()
    uv_tx[1] = gather_row((ue, ve), rows - 1)
    flows(late, rows, True, (ue, ve), (bu, bv), 0, True)
    for r in range(late, rows, 8):
        f = forcing(r, late, rows)
        if r > late:
            basis[0, pl.ds(WEST + r, 8)] = f
        else:
            f = jnp.where(top, jnp.broadcast_to(tu[pl.ds(rows - 1, 1)], (8, lanes)), f)
        fw_tx[pl.ds(r - late, 8)] = f
    loads[4].wait()
    for r in range(0, rows, 8):
        a = 0.5 * (own * (6.0 + de[pl.ds(r, 8)]) + (1.0 - own)) - 2.0
        a4[pl.ds(WEST + r, 8)] = a
        if r >= late:
            aw_tx[pl.ds(r - late, 8)] = jnp.where(top, own, a) if r == late else a
        if r < EAST:
            ae_tx[pl.ds(r, 8)] = jnp.where(bottom, own, a) if r + 8 == EAST else a

    pl.semaphore_wait(barrier, n - 1)

    def send(k, src, dst, to):
        copy = pltpu.make_async_remote_copy(
            src_ref=src, dst_ref=dst, send_sem=ssem.at[k], recv_sem=rsem.at[k],
            device_id={"blk": to}, device_id_type=pl.DeviceIdType.MESH,
        )
        copy.start()
        return copy

    sent = {}
    sent[0] = send(0, fw_tx, fw_rx, right)
    sent[1] = send(1, uv_tx.at[1], uv_rx.at[0], right)
    sent[2] = send(2, aw_tx, a4.at[pl.ds(0, WEST)], right)

    for k in (5, 6):
        loads[k].wait()
    uv_tx[0] = gather_row((ue, ve), 0)
    sent[3] = send(3, uv_tx.at[0], uv_rx.at[1], left)
    sent[4] = send(4, ae_tx, a4.at[pl.ds(WEST + rows, EAST)], left)
    flows(0, late, True, (ue, ve), (bu, bv), 0, True)
    for r in range(0, late + 8, 8):
        f = forcing(r, 0, rows)
        basis[0, pl.ds(WEST + r, 8)] = f
        if r < EAST:
            if r + 8 == EAST:
                f = jnp.where(bottom, jnp.broadcast_to(tu[pl.ds(0, 1)], (8, lanes)), f)
            fe_tx[pl.ds(r, 8)] = f
    sent[5] = send(5, fe_tx, fe_rx, left)
    for k in (7, 8):
        loads[k].wait()
    hs_tx[0] = gather_row((he, se), 0)
    hs_tx[1] = gather_row((he, se), rows - 1)
    sent[6] = send(6, hs_tx.at[1], hs_rx.at[0], right)
    sent[7] = send(7, hs_tx.at[0], hs_rx.at[1], left)

    window = (-SHIFT, rows - SHIFT)

    def in_window(r, x):
        if r < window[0]:
            return jnp.where(sub >= window[0] - r, x, 0.0)
        if r + 8 > window[1]:
            return jnp.where(sub < window[1] - r, x, 0.0)
        return x

    def fold(x):
        return tree([x[:, c : c + 128] for c in range(0, lanes, 128)])

    def sweep(p, first, last, low, high, wet, summed):
        known = {}

        def block(r):
            if r not in known:
                k0 = basis[p, pl.ds(WEST + r, 8)]
                m = wet(r) * k0
                known[r] = (k0, m, down_one(m), up_one(m))
            return known[r]

        squares, crosses, lasts = [], [], []
        for r in range(first, last, 8):
            k0, m, down, up = block(r)
            prior = block(r - 8)[2] if r > low else down
            after = block(r + 8)[3] if r + 8 < high else up
            vert = jnp.where(top, prior, down) + jnp.where(bottom, after, up)
            north, south = sides(m + 0.5 * vert)
            here = pl.ds(WEST + r, 8)
            half = a4[here] * k0 - (0.5 * wet(r)) * (vert + (north + south))
            new = 0.5 * half if p == 0 else half - basis[p - 1, here]
            basis[p + 1, here] = new
            if summed[0] <= r < summed[1]:
                kept = in_window(r, k0)
                squares.append(kept * kept)
                crosses.append(kept * in_window(r, new))
                if p + 1 == SWEEPS:
                    lasts.append(in_window(r, new) * in_window(r, new))
        return [tree([fold(t) for t in x]) for x in (squares, crosses, lasts) if x]

    def floor8(x):
        return x // 8 * 8

    def ceil8(x):
        return -(-x // 8) * 8

    inner_from, inner_to = ceil8(SWEEPS + 2), rows - SHIFT
    for p in range(SWEEPS):
        j = p + 1
        sums = sweep(
            p, floor8(2 + j), ceil8(rows - 2 - j), 0, rows, lambda r: own, (inner_from, inner_to)
        )
        for i, x in enumerate(sums):
            acc[2 * p + i] = x

    flows(0, rows, True, (he, se), (bh, bs), 2, False)

    def total_of(x):
        for step in (4, 2, 1):
            x = x + pltpu.roll(x, step, 0)
        return x

    def face(low, high, both):
        twice = [jnp.where(sub < levels, x, pltpu.roll(x, levels, 0)) for x in (low, high)]
        return 0.5 * (twice[0] + twice[1]) * both

    def seam(uv_low, uv_high, wet_low, wet_high, tu_low, tu_high, f_low, f_high):
        speed = face(uv_low, uv_high, wet_low * wet_high)
        flux = speed * jnp.where(speed > 0.0, uv_low, uv_high)
        term = level_weight * flux
        gu = total_of(jnp.where(sub < levels, term, 0.0))
        gv = total_of(jnp.where(sub < levels, 0.0, term))
        low_u, high_u = (-COURANT * wet_low) * gu, (COURANT * wet_high) * gu
        low_v, high_v = (-COURANT * wet_low) * gv, (COURANT * wet_high) * gv
        north, south = sides(jnp.where(sub < 4, high_v, low_v))
        across = north - south
        f_low = f_low + (0.5 * wet_low) * jnp.where(
            sub == 7, (tu_high + high_u) + across, jnp.where(sub == 6, low_u, 0.0)
        )
        f_high = f_high + (0.5 * wet_high) * jnp.where(
            sub == 0, across - (tu_low + low_u), jnp.where(sub == 1, -high_u, 0.0)
        )
        return speed, flux, f_low, f_high

    def row_of(ref, row):
        return jnp.broadcast_to(ref[pl.ds(row, 1)], (8, lanes))

    for k in (0, 1, 2):
        sent[k].wait_recv()
    west = row_of(a4, 0)
    speed_w, flux_w, f_low, f_high = seam(
        uv_rx[0], uv_tx[0], west, own, row_of(fw_rx, 0), row_of(tu, 0),
        fw_rx[pl.ds(WEST - 8, 8)], basis[0, pl.ds(WEST, 8)],
    )
    for r in range(0, WEST - 8, 8):
        basis[0, pl.ds(r, 8)] = fw_rx[pl.ds(r, 8)]
    basis[0, pl.ds(WEST - 8, 8)] = f_low
    basis[0, pl.ds(WEST, 8)] = f_high

    moments = [None] * MOMENTS
    base = [None, None]
    for p in range(SWEEPS):
        j = p + 1
        sums = sweep(
            p, floor8(j - 2 * SWEEPS - 2), ceil8(2 + j) if j < SWEEPS else inner_from, -WEST, rows,
            lambda r: west if r < 0 else own, (floor8(-SHIFT), 8),
        )
        for i, x in enumerate(sums):
            moments[2 * p + i] = x
        tail = []
        for r in range(8, inner_from, 8):
            k0, k1 = basis[p, pl.ds(WEST + r, 8)], basis[p + 1, pl.ds(WEST + r, 8)]
            tail.append((k0 * k0, k0 * k1) + ((k1 * k1,) if j == SWEEPS else ()))
        for i in range(len(sums)):
            moments[2 * p + i] = tree(
                [moments[2 * p + i], acc[2 * p + i]] + [fold(t[i]) for t in tail]
            )
    base = moments[:2]
    moments = base + [2.0 * x - base[i % 2] for i, x in enumerate(moments[2:])]
    spread = jnp.zeros((8, 128), F32)
    for i, x in enumerate(moments):
        spread = jnp.where(lane[:, :128] == i, jnp.sum(x, axis=1, keepdims=True), spread)
    slots[me] = jnp.sum(spread, axis=0, keepdims=True)
    copies = []
    for k in range(1, n):
        copy = pltpu.make_async_remote_copy(
            src_ref=slots.at[me], dst_ref=slots.at[me],
            send_sem=gs_sem.at[k], recv_sem=gr_sem.at[k],
            device_id={"blk": lax.rem(me + k, n)}, device_id_type=pl.DeviceIdType.MESH,
        )
        copy.start()
        copies.append(copy)

    for k in (3, 4, 5):
        sent[k].wait_recv()
    east = row_of(a4, WEST + rows + EAST - 1)
    speed_e, flux_e, f_low, f_high = seam(
        uv_tx[1], uv_rx[1], own, east, row_of(tu, rows - 1), row_of(fe_rx, EAST - 1),
        basis[0, pl.ds(WEST + rows - 8, 8)], fe_rx[pl.ds(0, 8)],
    )
    basis[0, pl.ds(WEST + rows - 8, 8)] = f_low
    basis[0, pl.ds(WEST + rows, 8)] = f_high
    for r in range(8, EAST, 8):
        basis[0, pl.ds(WEST + rows + r, 8)] = fe_rx[pl.ds(r, 8)]
    for p in range(SWEEPS):
        j = p + 1
        sweep(
            p, floor8(rows - 2 - j), ceil8(rows + SWEEPS - j), 0, rows + EAST,
            lambda r: own if r < rows else east, (0, 0),
        )

    for k in (6, 7):
        sent[k].wait_recv()

    def mend(outs, fixed, row):
        block, place = row // 8 * 8, row % 8
        for i, out in enumerate(outs):
            for level in range(levels):
                spot = i * levels + level
                old = out[level, pl.ds(block, 8)].astype(F32)
                x = pltpu.roll(fixed, (place - spot) % 8, 0) if (place - spot) % 8 else fixed
                out[level, pl.ds(block, 8)] = jnp.where(sub == place, x, old).astype(BF16)

    def carried(speed, low, high):
        return speed * jnp.where(speed > 0.0, low, high)

    mend((bu, bv), edges[0] + (COURANT * own) * flux_w, 0)
    mend((bu, bv), edges[1] - (COURANT * own) * flux_e, rows - 1)
    mend((bh, bs), edges[2] + (COURANT * own) * carried(speed_w, hs_rx[0], hs_tx[0]), 0)
    mend((bh, bs), edges[3] - (COURANT * own) * carried(speed_e, hs_tx[1], hs_rx[1]), rows - 1)

    for k in range(1, n):
        src = lax.rem(me + n - k, n)
        pltpu.make_async_remote_copy(
            src_ref=slots.at[src], dst_ref=slots.at[src],
            send_sem=gs_sem.at[k], recv_sem=gr_sem.at[k],
            device_id={"blk": src}, device_id_type=pl.DeviceIdType.MESH,
        ).wait_recv()
    mom[...] = jnp.broadcast_to(tree([slots[i] for i in range(n)]), (8, 128))
    for copy in copies:
        copy.wait_send()
    for copy in sent.values():
        copy.wait_send()


def finish(bh, bs, bu, bv, basis, mom, o_heat, o_salt, o_u, o_v, o_height, o_resid, hgt, res, sems):
    rows, lanes = hgt.shape
    stores = [
        pltpu.make_async_copy(src, dst, sems.at[i])
        for i, (src, dst) in enumerate(((bh, o_heat), (bs, o_salt), (bu, o_u), (bv, o_v)))
    ]
    for store in stores:
        store.start()
    row = mom[...]
    m = [jnp.broadcast_to(row[:, i : i + 1], (8, 128)) for i in range(MOMENTS)]
    gram = [[m[a + b] + m[abs(a - b)] for b in range(FIELDS)] for a in range(FIELDS)]
    offset, resid = inner_steps(gram, SWEEPS)

    def combine(vals, coef):
        return tree([c * v for v, c in zip(vals, coef) if c is not None])

    parts = 2
    step = rows // 8 // parts
    for part in range(parts):
        for s in range(part * step, (part + 1) * step):
            r = 8 * s
            for c in range(0, lanes, 128):
                vals = [basis[i, pl.ds(WEST + r, 8), c : c + 128] for i in range(FIELDS)]
                hgt[pl.ds(r, 8), c : c + 128] = combine(vals, offset)
                res[pl.ds(r, 8), c : c + 128] = combine(vals, resid)
        span = pl.ds(part * step * 8, step * 8)
        for i, (src, dst) in enumerate(((hgt, o_height), (res, o_resid))):
            store = pltpu.make_async_copy(src.at[span], dst.at[span], sems.at[4 + 2 * part + i])
            store.start()
            stores.append(store)
    for store in stores:
        store.wait()


def on_device(heat, salt, uvel, vvel, spacing, damp, flags):
    n = lax.axis_size("blk")
    levels, rows, lanes = uvel.shape
    total = WEST + rows + EAST
    hbm = pl.BlockSpec(memory_space=pltpu.HBM)
    vmem = pl.BlockSpec(memory_space=pltpu.VMEM)
    args = [
        pltpu.with_memory_space_constraint(x, pltpu.HBM)
        for x in (heat, salt, uvel, vvel, spacing, damp, flags)
    ]
    vm = pltpu.VMEM
    half = jax.ShapeDtypeStruct((levels, rows, lanes), BF16)
    flat = jax.ShapeDtypeStruct((rows, lanes), F32)
    full = vm((levels, rows, lanes), F32)
    dma = pltpu.SemaphoreType.DMA
    mids = (
        half, half, half, half,
        jax.ShapeDtypeStruct((FIELDS, total, lanes), F32),
        jax.ShapeDtypeStruct((8, 128), F32),
    )
    results = pl.pallas_call(
        functools.partial(kernel, n),
        out_shape=mids,
        in_specs=[hbm] * 7,
        out_specs=(vmem,) * 6,
        scratch_shapes=[
            full, full, full, full, full, full,
            vm((rows, lanes), F32),
            vm((rows, lanes), F32),
            vm((rows, lanes), F32),
            vm((MOMENTS, 8, 128), F32),
            vm((4, 8, lanes), F32),
            vm((2, 8, lanes), F32),
            vm((2, 8, lanes), F32),
            vm((2, 8, lanes), F32),
            vm((2, 8, lanes), F32),
            vm((WEST, lanes), F32),
            vm((EAST, lanes), F32),
            vm((total, lanes), F32),
            vm((WEST, lanes), F32),
            vm((EAST, lanes), F32),
            vm((WEST, lanes), F32),
            vm((EAST, lanes), F32),
            vm((n, 1, 128), F32),
            pltpu.SMEM(spacing.shape, F32),
            pltpu.SMEM(flags.shape, flags.dtype),
            dma((9,)),
            dma((8,)),
            dma((8,)),
            dma((n,)),
            dma((n,)),
        ],
        compiler_params=pltpu.CompilerParams(
            collective_id=0, has_side_effects=True, vmem_limit_bytes=40 * 1024 * 1024
        ),
    )(*args)
    results = [pltpu.with_memory_space_constraint(x, pltpu.VMEM) for x in results]
    shapes = (half, half, half, half, flat, flat)
    return pl.pallas_call(
        finish,
        out_shape=tuple(pltpu.HBM(x.shape, x.dtype) for x in shapes),
        in_specs=[vmem] * 6,
        out_specs=(hbm,) * 6,
        scratch_shapes=[vm((rows, lanes), F32), vm((rows, lanes), F32), dma((8,))],
        compiler_params=pltpu.CompilerParams(vmem_limit_bytes=8 * 1024 * 1024),
    )(*results)


def solution(mesh):
    return jax.shard_map(
        on_device,
        mesh=mesh,
        in_specs=(
            P("member", "blk", None),
            P("member", "blk", None),
            P("member", "blk", None),
            P("member", "blk", None),
            P(),
            P("blk", None),
            P("blk", None),
        ),
        out_specs=(
            P("member", "blk", None),
            P("member", "blk", None),
            P("member", "blk", None),
            P("member", "blk", None),
            P(("member", "blk"), None),
            P(("member", "blk"), None),
        ),
        check_vma=False,
    )
```

profile of v0, /device:TPU:0, one launch (start us, length us, event | category | flops | bytes accessed | tf_op | source)
XLA Modules:
  0.0 27.7 jit_solution(12964260519101958588)
XLA Ops:
  0.6 25.3 %shard_map.118 = (bf16[4,96,512]{2,1,0:T(8,128)(2,1)S(1)}, bf16[4,96,512]{2,1,0:T(8,128)(2,1)S(1)}, bf16[4,96,512]{2,1,0:T(8,128)(2,1)S(1)}, bf16[4,96,512]{2,1,...) custom-call(f32[4,96,512]{2,1,0:T(8,128)} %heat.1, f32[4,96,512]{2,1,0:T(8,128)} %salt.1, ...), custom_call_target="tpu_custom_call" | custom-call | tf_op jit(solution)/shard_map/pallas_call | solution.py:559
  25.9 1.8 %shard_map.119 = (bf16[4,96,512]{2,1,0:T(8,128)(2,1)}, bf16[4,96,512]{2,1,0:T(8,128)(2,1)}, bf16[4,96,512]{2,1,0:T(8,128)(2,1)}, bf16[4,96,512]{2,1,0:T(8,128)(2...) custom-call(bf16[4,96,512]{2,1,0:T(8,128)(2,1)S(1)} %get-tuple-element.12.bh, bf16[4,96,512]{2,1,0:T(8,128)(2,1)S(1)} %get-tuple-element.13.bs, ...), custom_call_target="tpu_custom_call" | custom-call | tf_op jit(solution)/shard_map/pallas_call | solution.py:597
where the time goes:
time: 27.9 us; the launch traced here: 27.7 us
  Pallas kernels  27.1 us (97%)
  between operations  0.64 us (2%)
    pallas_call x1, Pallas kernels, on_device(): pl.pallas_call(functools.partial(kernel, n), out_shape=mids, in_specs=[hb...  25.3 us
    pallas_call x1, Pallas kernels, on_device(): pl.pallas_call(finish, out_shape=tuple((pltpu.HBM(x.shape, x.dtype) for x...  1.82 us

commit v1 on v0

--- a/solution.py
+++ b/solution.py
@@ -93,7 +93,7 @@
     n,
     heat, salt, uvel, vvel, spacing, damp, flags,
     bh, bs, bu, bv, basis, mom,
-    ue, ve, he, se, ef, nf, de, tu, tv, acc, edges,
+    ue, ve, he, se, ef, nf, ff, de, tu, tv, acc, edges,
     uv_tx, hs_tx, uv_rx, hs_rx, aw_tx, ae_tx, a4, fw_tx, fe_tx, fw_rx, fe_rx, slots,
     space, marks,
     lsem, ssem, rsem, gs_sem, gr_sem,
@@ -186,52 +186,53 @@
     def pick(packed, block, spot, place):
         return jnp.where(sub == spot, pltpu.roll(block, (spot - place) % 8, 0) if (spot - place) % 8 else block, packed)
 
-    def advect(q, fe, fw, fn):
-        return own * (q - (0.5 * COURANT) * ((fe - fw) + (fn - south_of(fn))))
-
-    def flows(first, last, fresh, fields, outs, slot, keep):
-        u_like = fields[0]
+    def north_flux(first, last, fields, keep):
+        for level in range(levels):
+            for r in range(first, last, 8):
+                here = pl.ds(r, 8)
+                q0 = [ref[level, here] for ref in fields]
+                qn = [north_of(q) for q in q0]
+                if keep:
+                    north = (q0[1] + qn[1]) * ahead
+                    nf[level, here] = north
+                else:
+                    north = nf[level, here]
+                for i in range(2):
+                    ff[i, level, here] = north * jnp.where(north > 0.0, q0[i], qn[i])
+
+    def flows(first, last, fields, outs, slot, keep):
         ends = [zero, zero]
         for level in range(levels):
-            def east_of(r):
+            def ahead_of(ref, r, q0):
+                if r + 8 < rows:
+                    return jnp.where(bottom, up_one(ref[level, pl.ds(r + 8, 8)]), up_one(q0))
+                return up_one(q0)
+
+            def east_fluxes(r):
+                q0 = [ref[level, pl.ds(r, 8)] for ref in fields]
+                qp = [ahead_of(ref, r, q) for ref, q in zip(fields, q0)]
                 if keep:
-                    u0 = u_like[level, pl.ds(r, 8)]
-                    if r + 8 < rows:
-                        return u0 + jnp.where(bottom, up_one(u_like[level, pl.ds(r + 8, 8)]), up_one(u0))
-                    return jnp.where(bottom, 0.0, u0 + up_one(u0))
-                return ef[level, pl.ds(r, 8)]
-
-            def flux(ref, r, east):
-                q0 = ref[level, pl.ds(r, 8)]
-                qp = up_one(q0)
-                if r + 8 < rows:
-                    qp = jnp.where(bottom, up_one(ref[level, pl.ds(r + 8, 8)]), qp)
-                return q0, east * jnp.where(east > 0.0, q0, qp)
-
-            if first == 0:
-                before = [zero, zero]
-            else:
-                e = east_of(first - 8)
-                before = [down_one(flux(ref, first - 8, e)[1]) for ref in fields]
+                    east = q0[0] + qp[0]
+                    if r + 8 == rows:
+                        east = jnp.where(bottom, 0.0, east)
+                    ef[level, pl.ds(r, 8)] = east
+                else:
+                    east = ef[level, pl.ds(r, 8)]
+                return q0, [east * jnp.where(east > 0.0, a, b) for a, b in zip(q0, qp)]
+
+            before = [zero, zero] if first == 0 else [down_one(f) for f in east_fluxes(first - 8)[1]]
             pending = None
             for r in range(first, last, 8):
                 here = pl.ds(r, 8)
-                east = east_of(r)
-                if keep:
-                    v0 = fields[1][level, here]
-                    north = (v0 + north_of(v0)) * ahead
-                    ef[level, here] = east
-                    nf[level, here] = north
-                else:
-                    north = nf[level, here]
+                q0, fe = east_fluxes(r)
                 news = []
-                for i, ref in enumerate(fields):
-                    q0, fe = flux(ref, r, east)
-                    shifted = down_one(fe)
+                for i in range(2):
+                    shifted = down_one(fe[i])
                     fw = jnp.where(top, before[i], shifted)
                     before[i] = shifted
-                    fn = north * jnp.where(north > 0.0, q0, north_of(q0))
-                    new = advect(q0, fe, fw, fn)
+                    fn = ff[i, level, here]
+                    spread = (fe[i] - fw) + (fn - south_of(fn))
+                    new = own * (q0[i] - (0.5 * COURANT) * spread)
                     news.append(new)
                     if keep:
                         total = (tu, tv)[i]
@@ -263,7 +264,8 @@
     for k in (2, 3):
         loads[k].wait()
     uv_tx[1] = gather_row((ue, ve), rows - 1)
-    flows(late, rows, True, (ue, ve), (bu, bv), 0, True)
+    north_flux(late, rows, (ue, ve), True)
+    flows(late, rows, (ue, ve), (bu, bv), 0, True)
     for r in range(late, rows, 8):
         f = forcing(r, late, rows)
         if r > late:
@@ -300,7 +302,8 @@
     uv_tx[0] = gather_row((ue, ve), 0)
     sent[3] = send(3, uv_tx.at[0], uv_rx.at[1], left)
     sent[4] = send(4, ae_tx, a4.at[pl.ds(WEST + rows, EAST)], left)
-    flows(0, late, True, (ue, ve), (bu, bv), 0, True)
+    north_flux(0, late, (ue, ve), True)
+    flows(0, late, (ue, ve), (bu, bv), 0, True)
     for r in range(0, late + 8, 8):
         f = forcing(r, 0, rows)
         basis[0, pl.ds(WEST + r, 8)] = f
@@ -372,7 +375,8 @@
         for i, x in enumerate(sums):
             acc[2 * p + i] = x
 
-    flows(0, rows, True, (he, se), (bh, bs), 2, False)
+    north_flux(0, rows, (he, se), False)
+    flows(0, rows, (he, se), (bh, bs), 2, False)
 
     def total_of(x):
         for step in (4, 2, 1):
@@ -563,6 +567,7 @@
         out_specs=(vmem,) * 6,
         scratch_shapes=[
             full, full, full, full, full, full,
+            vm((2, levels, rows, lanes), F32),
             vm((rows, lanes), F32),
             vm((rows, lanes), F32),
             vm((rows, lanes), F32),

time: 27.9 us -> 18.1 us (0.65)
  Pallas kernels: 27.1 us -> 17.3 us
    pallas_call x1, Pallas kernels: 25.3 us -> 15.5 us  [on_device(): pl.pallas_call(functools.partial(kernel, n), out_shape=mids, in_specs=[hb...]
where the time goes in v1:
time: 18.1 us; the launch traced here: 18 us
  Pallas kernels  17.3 us (96%)
  between operations  0.64 us (4%)
    pallas_call x1, Pallas kernels, on_device(): pl.pallas_call(functools.partial(kernel, n), out_shape=mids, in_specs=[hb...  15.5 us
    pallas_call x1, Pallas kernels, on_device(): pl.pallas_call(finish, out_shape=tuple((pltpu.HBM(x.shape, x.dtype) for x...  1.82 us

profile of v1, /device:TPU:0, one launch (start us, length us, event | category | flops | bytes accessed | tf_op | source)
XLA Modules:
  0.0 18.0 jit_solution(8321414426650697383)
XLA Ops:
  0.6 15.5 %shard_map.118 = (bf16[4,96,512]{2,1,0:T(8,128)(2,1)S(1)}, bf16[4,96,512]{2,1,0:T(8,128)(2,1)S(1)}, bf16[4,96,512]{2,1,0:T(8,128)(2,1)S(1)}, bf16[4,96,512]{2,1,...) custom-call(f32[4,96,512]{2,1,0:T(8,128)} %heat.1, f32[4,96,512]{2,1,0:T(8,128)} %salt.1, ...), custom_call_target="tpu_custom_call" | custom-call | tf_op jit(solution)/shard_map/pallas_call | solution.py:563
  16.1 1.8 %shard_map.119 = (bf16[4,96,512]{2,1,0:T(8,128)(2,1)}, bf16[4,96,512]{2,1,0:T(8,128)(2,1)}, bf16[4,96,512]{2,1,0:T(8,128)(2,1)}, bf16[4,96,512]{2,1,0:T(8,128)(2...) custom-call(bf16[4,96,512]{2,1,0:T(8,128)(2,1)S(1)} %get-tuple-element.12.bh, bf16[4,96,512]{2,1,0:T(8,128)(2,1)S(1)} %get-tuple-element.13.bs, ...), custom_call_target="tpu_custom_call" | custom-call | tf_op jit(solution)/shard_map/pallas_call | solution.py:602

commit v2 on v1

--- a/solution.py
+++ b/solution.py
@@ -69,7 +69,7 @@
     along = [one] + [None] * sweeps
     resid = [one] + [None] * sweeps
     offset = [None] * extent
-    norm_now = quadratic(gram, resid, resid)
+    norm_now = gram[0][0]
     for sweep in range(sweeps):
         image = []
         for i in range(extent):
@@ -78,12 +78,13 @@
                 if table[i, j] != 0.0:
                     total = plus(total, scaled(float(table[i, j]), along[j]))
             image.append(total)
+        scale = 1.0 / norm_now
         alpha = norm_now / quadratic(gram, along, image)
         offset = [plus(o, scaled(alpha, a)) for o, a in zip(offset, along)]
         resid = [plus(r, scaled(-alpha, a)) for r, a in zip(resid, image)]
         if sweep + 1 < sweeps:
             norm_next = quadratic(gram, resid, resid)
-            beta = norm_next / norm_now
+            beta = norm_next * scale
             along = [plus(r, scaled(beta, a)) for r, a in zip(resid, along)]
             norm_now = norm_next
     return offset, resid
@@ -96,7 +97,7 @@
     ue, ve, he, se, ef, nf, ff, de, tu, tv, acc, edges,
     uv_tx, hs_tx, uv_rx, hs_rx, aw_tx, ae_tx, a4, fw_tx, fe_tx, fw_rx, fe_rx, slots,
     space, marks,
-    lsem, ssem, rsem, gs_sem, gr_sem,
+    flux_e, lsem, ssem, rsem, gsem, late_sem,
 ):
     levels, rows, lanes = ue.shape
     me = lax.axis_index("blk")
@@ -109,26 +110,48 @@
             ref.at[:, pl.ds(lo, hi - lo)], buf.at[:, pl.ds(lo, hi - lo)], lsem.at[sem]
         )
 
+    def pair(lo, hi, sem):
+        both = ff.at[:, :, pl.ds(lo, hi - lo)]
+        return pltpu.make_async_copy(both, both, lsem.at[sem])
+
     loads = [
         pltpu.make_async_copy(flags, marks, lsem.at[0]),
         pltpu.make_async_copy(spacing, space, lsem.at[1]),
         part(uvel, ue, split, rows, 2),
-        part(vvel, ve, split, rows, 3),
-        pltpu.make_async_copy(damp, de, lsem.at[4]),
-        part(uvel, ue, 0, split, 5),
-        part(vvel, ve, 0, split, 6),
-        pltpu.make_async_copy(heat, he, lsem.at[7]),
-        pltpu.make_async_copy(salt, se, lsem.at[8]),
+        part(vvel, ve, split, rows, 2),
+        pltpu.make_async_copy(damp, de, lsem.at[3]),
+        part(uvel, ue, 0, split, 4),
+        part(vvel, ve, 0, split, 4),
     ]
-    for load in loads:
+    more = [
+        pltpu.make_async_copy(heat, he, lsem.at[5]),
+        pltpu.make_async_copy(salt, se, lsem.at[5]),
+    ]
+    for load in loads[:4]:
         load.start()
 
     barrier = pltpu.get_barrier_semaphore()
+
+    def tell(sem, to):
+        pl.semaphore_signal(
+            sem, inc=1, device_id={"blk": to}, device_id_type=pl.DeviceIdType.MESH
+        )
+
+    at_start, at_end = me == 0, me == n - 1
+    pl.when(me > 0)(lambda: tell(barrier, left))
     for k in range(1, n):
-        pl.semaphore_signal(
-            barrier, inc=1, device_id={"blk": lax.rem(me + k, n)},
-            device_id_type=pl.DeviceIdType.MESH,
-        )
+        pl.when(me + k < n)(functools.partial(tell, barrier, lax.rem(me + k, n)))
+    for load in loads[4:]:
+        load.start()
+
+    def pass_barrier():
+        pl.semaphore_wait(barrier, jnp.where(at_end, n - 1, me + 1))
+        for k in range(2, n):
+            pl.when(me - k >= 0)(functools.partial(tell, late_sem.at[0], lax.rem(me + n - k, n)))
+
+    def hear_late():
+        later = n - 2 - me
+        pl.when(later > 0)(lambda: pl.semaphore_wait(late_sem.at[0], later))
 
     lane = lax.broadcasted_iota(jnp.int32, (8, lanes), 1)
     sub = lax.broadcasted_iota(jnp.int32, (8, lanes), 0)
@@ -261,9 +284,39 @@
         prior = jnp.where(top, down_one(tu[pl.ds(r - 8, 8)]) if r > low else 0.0, down_one(x0))
         return (0.5 * own) * ((after - prior) + (north - south))
 
-    for k in (2, 3):
-        loads[k].wait()
+    def send(src, dst, sem, to):
+        pltpu.make_async_remote_copy(
+            src_ref=src, dst_ref=dst, send_sem=ssem.at[0], recv_sem=rsem.at[sem],
+            device_id={"blk": to}, device_id_type=pl.DeviceIdType.MESH,
+        ).start()
+
+    def arrive(sem, height):
+        lot = a4.at[pl.ds(0, height)]
+        pltpu.make_async_remote_copy(
+            src_ref=lot, dst_ref=lot, send_sem=ssem.at[0], recv_sem=rsem.at[sem],
+            device_id={"blk": right}, device_id_type=pl.DeviceIdType.MESH,
+        ).wait_recv()
+
+    def send_left():
+        send(uv_tx.at[0], uv_rx.at[1], 1, left)
+        send(ae_tx, a4.at[pl.ds(WEST + rows, EAST)], 1, left)
+        send(fe_tx, fe_rx, 1, left)
+
+    pair(split, rows, 2).wait()
+    for load in more:
+        load.start()
     uv_tx[1] = gather_row((ue, ve), rows - 1)
+    loads[4].wait()
+    for r in range(0, rows, 8):
+        a = 0.5 * (own * (6.0 + de[pl.ds(r, 8)]) + (1.0 - own)) - 2.0
+        a4[pl.ds(WEST + r, 8)] = a
+        if r >= late:
+            aw_tx[pl.ds(r - late, 8)] = jnp.where(top, own, a) if r == late else a
+        if r < EAST:
+            ae_tx[pl.ds(r, 8)] = jnp.where(bottom, own, a) if r + 8 == EAST else a
+    pass_barrier()
+    send(uv_tx.at[1], uv_rx.at[0], 0, right)
+    send(aw_tx, a4.at[pl.ds(0, WEST)], 0, right)
     north_flux(late, rows, (ue, ve), True)
     flows(late, rows, (ue, ve), (bu, bv), 0, True)
     for r in range(late, rows, 8):
@@ -273,35 +326,10 @@
         else:
             f = jnp.where(top, jnp.broadcast_to(tu[pl.ds(rows - 1, 1)], (8, lanes)), f)
         fw_tx[pl.ds(r - late, 8)] = f
-    loads[4].wait()
-    for r in range(0, rows, 8):
-        a = 0.5 * (own * (6.0 + de[pl.ds(r, 8)]) + (1.0 - own)) - 2.0
-        a4[pl.ds(WEST + r, 8)] = a
-        if r >= late:
-            aw_tx[pl.ds(r - late, 8)] = jnp.where(top, own, a) if r == late else a
-        if r < EAST:
-            ae_tx[pl.ds(r, 8)] = jnp.where(bottom, own, a) if r + 8 == EAST else a
-
-    pl.semaphore_wait(barrier, n - 1)
-
-    def send(k, src, dst, to):
-        copy = pltpu.make_async_remote_copy(
-            src_ref=src, dst_ref=dst, send_sem=ssem.at[k], recv_sem=rsem.at[k],
-            device_id={"blk": to}, device_id_type=pl.DeviceIdType.MESH,
-        )
-        copy.start()
-        return copy
-
-    sent = {}
-    sent[0] = send(0, fw_tx, fw_rx, right)
-    sent[1] = send(1, uv_tx.at[1], uv_rx.at[0], right)
-    sent[2] = send(2, aw_tx, a4.at[pl.ds(0, WEST)], right)
-
-    for k in (5, 6):
-        loads[k].wait()
+    send(fw_tx, fw_rx, 0, right)
+
+    pair(0, split, 4).wait()
     uv_tx[0] = gather_row((ue, ve), 0)
-    sent[3] = send(3, uv_tx.at[0], uv_rx.at[1], left)
-    sent[4] = send(4, ae_tx, a4.at[pl.ds(WEST + rows, EAST)], left)
     north_flux(0, late, (ue, ve), True)
     flows(0, late, (ue, ve), (bu, bv), 0, True)
     for r in range(0, late + 8, 8):
@@ -311,13 +339,7 @@
             if r + 8 == EAST:
                 f = jnp.where(bottom, jnp.broadcast_to(tu[pl.ds(0, 1)], (8, lanes)), f)
             fe_tx[pl.ds(r, 8)] = f
-    sent[5] = send(5, fe_tx, fe_rx, left)
-    for k in (7, 8):
-        loads[k].wait()
-    hs_tx[0] = gather_row((he, se), 0)
-    hs_tx[1] = gather_row((he, se), rows - 1)
-    sent[6] = send(6, hs_tx.at[1], hs_rx.at[0], right)
-    sent[7] = send(7, hs_tx.at[0], hs_rx.at[1], left)
+    pl.when(me > 0)(send_left)
 
     window = (-SHIFT, rows - SHIFT)
 
@@ -375,8 +397,15 @@
         for i, x in enumerate(sums):
             acc[2 * p + i] = x
 
-    north_flux(0, rows, (he, se), False)
-    flows(0, rows, (he, se), (bh, bs), 2, False)
+    pltpu.make_async_copy(ff, ff, lsem.at[5]).wait()
+    hs_tx[0] = gather_row((he, se), 0)
+    hs_tx[1] = gather_row((he, se), rows - 1)
+    send(hs_tx.at[1], hs_rx.at[0], 2, right)
+    pl.when(me > 0)(lambda: send(hs_tx.at[0], hs_rx.at[1], 2, left))
+
+    def tracers():
+        north_flux(0, rows, (he, se), False)
+        flows(0, rows, (he, se), (bh, bs), 2, False)
 
     def total_of(x):
         for step in (4, 2, 1):
@@ -408,8 +437,37 @@
     def row_of(ref, row):
         return jnp.broadcast_to(ref[pl.ds(row, 1)], (8, lanes))
 
-    for k in (0, 1, 2):
-        sent[k].wait_recv()
+    def tracers_and_east(both=True):
+        if both:
+            tracers()
+        arrive(1, 2 * EAST + 8)
+        east = row_of(a4, WEST + rows + EAST - 1)
+        _, flux, f_low, f_high = seam(
+            uv_tx[1], uv_rx[1], own, east, row_of(tu, rows - 1), row_of(fe_rx, EAST - 1),
+            basis[0, pl.ds(WEST + rows - 8, 8)], fe_rx[pl.ds(0, 8)],
+        )
+        flux_e[...] = flux
+        basis[0, pl.ds(WEST + rows - 8, 8)] = f_low
+        basis[0, pl.ds(WEST + rows, 8)] = f_high
+        for r in range(8, EAST, 8):
+            basis[0, pl.ds(WEST + rows + r, 8)] = fe_rx[pl.ds(r, 8)]
+        for p in range(SWEEPS):
+            j = p + 1
+            sweep(
+                p, floor8(rows - 2 - j), ceil8(rows + SWEEPS - j), 0, rows + EAST,
+                lambda r: own if r < rows else east, (0, 0),
+            )
+
+    def before_west():
+        tracers()
+        hear_late()
+        send_left()
+        send(hs_tx.at[0], hs_rx.at[1], 2, left)
+        tracers_and_east(False)
+
+    pl.when(at_start)(before_west)
+
+    arrive(0, 2 * WEST + 8)
     west = row_of(a4, 0)
     speed_w, flux_w, f_low, f_high = seam(
         uv_rx[0], uv_tx[0], west, own, row_of(fw_rx, 0), row_of(tu, 0),
@@ -444,36 +502,16 @@
     for i, x in enumerate(moments):
         spread = jnp.where(lane[:, :128] == i, jnp.sum(x, axis=1, keepdims=True), spread)
     slots[me] = jnp.sum(spread, axis=0, keepdims=True)
-    copies = []
-    for k in range(1, n):
-        copy = pltpu.make_async_remote_copy(
+    pl.when(me > 0)(hear_late)
+    for k in range(n - 1):
+        pltpu.make_async_remote_copy(
             src_ref=slots.at[me], dst_ref=slots.at[me],
-            send_sem=gs_sem.at[k], recv_sem=gr_sem.at[k],
-            device_id={"blk": lax.rem(me + k, n)}, device_id_type=pl.DeviceIdType.MESH,
-        )
-        copy.start()
-        copies.append(copy)
-
-    for k in (3, 4, 5):
-        sent[k].wait_recv()
-    east = row_of(a4, WEST + rows + EAST - 1)
-    speed_e, flux_e, f_low, f_high = seam(
-        uv_tx[1], uv_rx[1], own, east, row_of(tu, rows - 1), row_of(fe_rx, EAST - 1),
-        basis[0, pl.ds(WEST + rows - 8, 8)], fe_rx[pl.ds(0, 8)],
-    )
-    basis[0, pl.ds(WEST + rows - 8, 8)] = f_low
-    basis[0, pl.ds(WEST + rows, 8)] = f_high
-    for r in range(8, EAST, 8):
-        basis[0, pl.ds(WEST + rows + r, 8)] = fe_rx[pl.ds(r, 8)]
-    for p in range(SWEEPS):
-        j = p + 1
-        sweep(
-            p, floor8(rows - 2 - j), ceil8(rows + SWEEPS - j), 0, rows + EAST,
-            lambda r: own if r < rows else east, (0, 0),
-        )
-
-    for k in (6, 7):
-        sent[k].wait_recv()
+            send_sem=gsem.at[0], recv_sem=gsem.at[1],
+            device_id={"blk": k + jnp.where(k >= me, 1, 0)}, device_id_type=pl.DeviceIdType.MESH,
+        ).start()
+
+    pl.when(me > 0)(tracers_and_east)
+    arrive(2, 16)
 
     def mend(outs, fixed, row):
         block, place = row // 8 * 8, row % 8
@@ -488,29 +526,32 @@
         return speed * jnp.where(speed > 0.0, low, high)
 
     mend((bu, bv), edges[0] + (COURANT * own) * flux_w, 0)
-    mend((bu, bv), edges[1] - (COURANT * own) * flux_e, rows - 1)
+    mend((bu, bv), edges[1] - (COURANT * own) * flux_e[...], rows - 1)
+    east = row_of(a4, WEST + rows + EAST - 1)
+    speed_e = face(uv_tx[1], uv_rx[1], own * east)
     mend((bh, bs), edges[2] + (COURANT * own) * carried(speed_w, hs_rx[0], hs_tx[0]), 0)
     mend((bh, bs), edges[3] - (COURANT * own) * carried(speed_e, hs_tx[1], hs_rx[1]), rows - 1)
 
-    for k in range(1, n):
-        src = lax.rem(me + n - k, n)
-        pltpu.make_async_remote_copy(
-            src_ref=slots.at[src], dst_ref=slots.at[src],
-            send_sem=gs_sem.at[k], recv_sem=gr_sem.at[k],
-            device_id={"blk": src}, device_id_type=pl.DeviceIdType.MESH,
-        ).wait_recv()
+    others = slots.at[pl.ds(0, n - 1)]
+    rest = pltpu.make_async_remote_copy(
+        src_ref=others, dst_ref=others, send_sem=gsem.at[0], recv_sem=gsem.at[1],
+        device_id={"blk": right}, device_id_type=pl.DeviceIdType.MESH,
+    )
+    rest.wait_recv()
     mom[...] = jnp.broadcast_to(tree([slots[i] for i in range(n)]), (8, 128))
-    for copy in copies:
-        copy.wait_send()
-    for copy in sent.values():
-        copy.wait_send()
+    rest.wait_send()
+    lot = a4.at[pl.ds(0, 2 * WEST + 2 * EAST + 32)]
+    pltpu.make_async_remote_copy(
+        src_ref=lot, dst_ref=lot, send_sem=ssem.at[0], recv_sem=rsem.at[0],
+        device_id={"blk": right}, device_id_type=pl.DeviceIdType.MESH,
+    ).wait_send()
 
 
 def finish(bh, bs, bu, bv, basis, mom, o_heat, o_salt, o_u, o_v, o_height, o_resid, hgt, res, sems):
     rows, lanes = hgt.shape
     stores = [
-        pltpu.make_async_copy(src, dst, sems.at[i])
-        for i, (src, dst) in enumerate(((bh, o_heat), (bs, o_salt), (bu, o_u), (bv, o_v)))
+        pltpu.make_async_copy(src, dst, sems.at[0])
+        for src, dst in ((bh, o_heat), (bs, o_salt), (bu, o_u), (bv, o_v))
     ]
     for store in stores:
         store.start()
@@ -532,12 +573,12 @@
                 hgt[pl.ds(r, 8), c : c + 128] = combine(vals, offset)
                 res[pl.ds(r, 8), c : c + 128] = combine(vals, resid)
         span = pl.ds(part * step * 8, step * 8)
-        for i, (src, dst) in enumerate(((hgt, o_height), (res, o_resid))):
-            store = pltpu.make_async_copy(src.at[span], dst.at[span], sems.at[4 + 2 * part + i])
-            store.start()
-            stores.append(store)
-    for store in stores:
-        store.wait()
+        for src, dst in ((hgt, o_height), (res, o_resid)):
+            pltpu.make_async_copy(src.at[span], dst.at[span], sems.at[1]).start()
+    levels = bh.shape[0]
+    for sem, count in ((0, 2 * levels), (1, 2)):
+        lot = basis.at[pl.ds(0, count), pl.ds(0, rows)]
+        pltpu.make_async_copy(lot, lot, sems.at[sem]).wait()
 
 
 def on_device(heat, salt, uvel, vvel, spacing, damp, flags):
@@ -587,11 +628,12 @@
             vm((n, 1, 128), F32),
             pltpu.SMEM(spacing.shape, F32),
             pltpu.SMEM(flags.shape, flags.dtype),
-            dma((9,)),
-            dma((8,)),
-            dma((8,)),
-            dma((n,)),
-            dma((n,)),
+            vm((8, lanes), F32),
+            dma((6,)),
+            dma((1,)),
+            dma((3,)),
+            dma((2,)),
+            pltpu.SemaphoreType.REGULAR((1,)),
         ],
         compiler_params=pltpu.CompilerParams(
             collective_id=0, has_side_effects=True, vmem_limit_bytes=40 * 1024 * 1024
@@ -604,7 +646,7 @@
         out_shape=tuple(pltpu.HBM(x.shape, x.dtype) for x in shapes),
         in_specs=[vmem] * 6,
         out_specs=(hbm,) * 6,
-        scratch_shapes=[vm((rows, lanes), F32), vm((rows, lanes), F32), dma((8,))],
+        scratch_shapes=[vm((rows, lanes), F32), vm((rows, lanes), F32), dma((2,))],
         compiler_params=pltpu.CompilerParams(vmem_limit_bytes=8 * 1024 * 1024),
     )(*results)
 

time: 18.1 us -> 16.5 us (0.912)
  Pallas kernels: 17.3 us -> 15.7 us
    pallas_call x1, Pallas kernels: 15.5 us -> 13.9 us  [on_device(): pl.pallas_call(functools.partial(kernel, n), out_shape=mids, in_specs=[hb...]
where the time goes in v2:
time: 16.5 us; the launch traced here: 16.3 us
  Pallas kernels  15.7 us (95%)
  between operations  0.64 us (4%)
    pallas_call x1, Pallas kernels, on_device(): pl.pallas_call(functools.partial(kernel, n), out_shape=mids, in_specs=[hb...  13.9 us
    pallas_call x1, Pallas kernels, on_device(): pl.pallas_call(finish, out_shape=tuple((pltpu.HBM(x.shape, x.dtype) for x...  1.76 us

profile of v2, /device:TPU:0, one launch (start us, length us, event | category | flops | bytes accessed | tf_op | source)
XLA Modules:
  0.0 16.3 jit_solution(15565817071561951498)
XLA Ops:
  0.6 13.9 %shard_map.118 = (bf16[4,96,512]{2,1,0:T(8,128)(2,1)S(1)}, bf16[4,96,512]{2,1,0:T(8,128)(2,1)S(1)}, bf16[4,96,512]{2,1,0:T(8,128)(2,1)S(1)}, bf16[4,96,512]{2,1,...) custom-call(f32[4,96,512]{2,1,0:T(8,128)} %heat.1, f32[4,96,512]{2,1,0:T(8,128)} %salt.1, ...), custom_call_target="tpu_custom_call" | custom-call | tf_op jit(solution)/shard_map/pallas_call | solution.py:604
  14.6 1.8 %shard_map.119 = (bf16[4,96,512]{2,1,0:T(8,128)(2,1)}, bf16[4,96,512]{2,1,0:T(8,128)(2,1)}, bf16[4,96,512]{2,1,0:T(8,128)(2,1)}, bf16[4,96,512]{2,1,0:T(8,128)(2...) custom-call(bf16[4,96,512]{2,1,0:T(8,128)(2,1)S(1)} %get-tuple-element.12.bh, bf16[4,96,512]{2,1,0:T(8,128)(2,1)S(1)} %get-tuple-element.13.bs, ...), custom_call_target="tpu_custom_call" | custom-call | tf_op jit(solution)/shard_map/pallas_call | solution.py:644

commit v3 on v2

--- a/solution.py
+++ b/solution.py
@@ -12,7 +12,7 @@
 CG_BLOCKS = 3
 SWEEPS = SSTEP * CG_BLOCKS
 FIELDS = SWEEPS + 1
-MOMENTS = 2 * SWEEPS + 1
+MOMENTS = 2 * SWEEPS
 COURANT = 0.2
 SHIFT = SWEEPS + 2
 WEST = -(-(2 * SWEEPS + 2) // 8) * 8
@@ -42,11 +42,13 @@
     return terms[0]
 
 
-def quadratic(gram, left, right):
+def square(even, coef):
     rows = []
-    for i, li in enumerate(left):
-        if li is not None:
-            rows.append(li * tree([gram[i][j] * rj for j, rj in enumerate(right) if rj is not None]))
+    for i, ci in enumerate(coef):
+        if ci is not None:
+            row = [(even[2 * i] + even[0]) * ci]
+            row += [2.0 * (even[i + j] + even[i - j]) * coef[j] for j in range(i)]
+            rows.append(ci * tree(row))
     return tree(rows)
 
 
@@ -62,14 +64,14 @@
     return None if a is None else scale * a
 
 
-def inner_steps(gram, sweeps):
+def inner_steps(moments, sweeps):
     extent = sweeps + 1
     table = shift_table(extent)
-    one = jnp.ones_like(gram[0][0])
+    one = jnp.ones_like(moments[0])
     along = [one] + [None] * sweeps
     resid = [one] + [None] * sweeps
     offset = [None] * extent
-    norm_now = gram[0][0]
+    norm_now = moments[0] + moments[0]
     for sweep in range(sweeps):
         image = []
         for i in range(extent):
@@ -79,11 +81,19 @@
                     total = plus(total, scaled(float(table[i, j]), along[j]))
             image.append(total)
         scale = 1.0 / norm_now
-        alpha = norm_now / quadratic(gram, along, image)
+        rows = []
+        for i, ai in enumerate(along):
+            if ai is not None:
+                row = [
+                    (moments[i + j] + moments[abs(i - j)]) * image[j]
+                    for j in range(extent) if image[j] is not None
+                ]
+                rows.append(ai * tree(row))
+        alpha = norm_now / tree(rows)
         offset = [plus(o, scaled(alpha, a)) for o, a in zip(offset, along)]
         resid = [plus(r, scaled(-alpha, a)) for r, a in zip(resid, image)]
         if sweep + 1 < sweeps:
-            norm_next = quadratic(gram, resid, resid)
+            norm_next = square(moments, resid)
             beta = norm_next * scale
             along = [plus(r, scaled(beta, a)) for r, a in zip(resid, along)]
             norm_now = norm_next
@@ -117,9 +127,9 @@
     loads = [
         pltpu.make_async_copy(flags, marks, lsem.at[0]),
         pltpu.make_async_copy(spacing, space, lsem.at[1]),
+        pltpu.make_async_copy(damp, de, lsem.at[3]),
         part(uvel, ue, split, rows, 2),
         part(vvel, ve, split, rows, 2),
-        pltpu.make_async_copy(damp, de, lsem.at[3]),
         part(uvel, ue, 0, split, 4),
         part(vvel, ve, 0, split, 4),
     ]
@@ -127,7 +137,7 @@
         pltpu.make_async_copy(heat, he, lsem.at[5]),
         pltpu.make_async_copy(salt, se, lsem.at[5]),
     ]
-    for load in loads[:4]:
+    for load in loads[:5]:
         load.start()
 
     barrier = pltpu.get_barrier_semaphore()
@@ -141,11 +151,13 @@
     pl.when(me > 0)(lambda: tell(barrier, left))
     for k in range(1, n):
         pl.when(me + k < n)(functools.partial(tell, barrier, lax.rem(me + k, n)))
-    for load in loads[4:]:
+    for load in loads[5:]:
         load.start()
 
     def pass_barrier():
         pl.semaphore_wait(barrier, jnp.where(at_end, n - 1, me + 1))
+
+    def tell_earlier():
         for k in range(2, n):
             pl.when(me - k >= 0)(functools.partial(tell, late_sem.at[0], lax.rem(me + n - k, n)))
 
@@ -166,6 +178,21 @@
 
     def sides(x):
         return jnp.where(lane == lanes - 1, 0.0, north_of(x)), jnp.where(lane == 0, 0.0, south_of(x))
+
+    slim = lane[:, :128]
+
+    def beside(x):
+        tiles = [x[:, c : c + 128] for c in range(0, lanes, 128)]
+        north = [pltpu.roll(t, 127, 1) for t in tiles] + [0.0]
+        south = [pltpu.roll(t, 1, 1) for t in tiles]
+        south = [0.0] + south
+        return jnp.concatenate(
+            [
+                jnp.where(slim == 127, north[i + 1], north[i]) + jnp.where(slim == 0, south[i], south[i + 1])
+                for i in range(len(tiles))
+            ],
+            axis=1,
+        )
 
     def up_one(x):
         return pltpu.roll(x, 7, 0)
@@ -181,6 +208,7 @@
     for k in range(tiles):
         own = jnp.where(lane_tile == k, marks[0, k].astype(F32), own)
     ahead = jnp.where(lane == lanes - 1, 0.0, own * north_of(own))
+    half_own = 0.5 * own
     whole_w = jnp.zeros((8, 128), F32)
     for j in range(levels):
         whole_w = whole_w + space[j]
@@ -302,11 +330,7 @@
         send(ae_tx, a4.at[pl.ds(WEST + rows, EAST)], 1, left)
         send(fe_tx, fe_rx, 1, left)
 
-    pair(split, rows, 2).wait()
-    for load in more:
-        load.start()
-    uv_tx[1] = gather_row((ue, ve), rows - 1)
-    loads[4].wait()
+    loads[2].wait()
     for r in range(0, rows, 8):
         a = 0.5 * (own * (6.0 + de[pl.ds(r, 8)]) + (1.0 - own)) - 2.0
         a4[pl.ds(WEST + r, 8)] = a
@@ -314,9 +338,14 @@
             aw_tx[pl.ds(r - late, 8)] = jnp.where(top, own, a) if r == late else a
         if r < EAST:
             ae_tx[pl.ds(r, 8)] = jnp.where(bottom, own, a) if r + 8 == EAST else a
+    pair(split, rows, 2).wait()
+    uv_tx[1] = gather_row((ue, ve), rows - 1)
     pass_barrier()
     send(uv_tx.at[1], uv_rx.at[0], 0, right)
     send(aw_tx, a4.at[pl.ds(0, WEST)], 0, right)
+    tell_earlier()
+    for load in more:
+        load.start()
     north_flux(late, rows, (ue, ve), True)
     flows(late, rows, (ue, ve), (bu, bv), 0, True)
     for r in range(late, rows, 8):
@@ -353,34 +382,42 @@
     def fold(x):
         return tree([x[:, c : c + 128] for c in range(0, lanes, 128)])
 
-    def sweep(p, first, last, low, high, wet, summed):
+    def sweep(p, first, last, low, high, half_wet, summed, held=None):
+        held = {} if held is None else held
         known = {}
+
+        def field(q, r):
+            return held[q, r] if (q, r) in held else basis[q, pl.ds(WEST + r, 8)]
 
         def block(r):
             if r not in known:
-                k0 = basis[p, pl.ds(WEST + r, 8)]
-                m = wet(r) * k0
-                known[r] = (k0, m, down_one(m), up_one(m))
+                k0 = field(p, r)
+                known[r] = (k0, down_one(k0), up_one(k0))
             return known[r]
 
-        squares, crosses, lasts = [], [], []
+        squares, crosses = [], []
+        turned = {}
         for r in range(first, last, 8):
-            k0, m, down, up = block(r)
-            prior = block(r - 8)[2] if r > low else down
-            after = block(r + 8)[3] if r + 8 < high else up
+            k0, down, up = block(r)
+            prior = block(r - 8)[1] if r > low else down
+            after = block(r + 8)[2] if r + 8 < high else up
             vert = jnp.where(top, prior, down) + jnp.where(bottom, after, up)
-            north, south = sides(m + 0.5 * vert)
+            turned[r] = vert, beside(k0 + 0.5 * vert)
+        for r in range(first, last, 8):
+            k0 = block(r)[0]
+            vert, side = turned[r]
             here = pl.ds(WEST + r, 8)
-            half = a4[here] * k0 - (0.5 * wet(r)) * (vert + (north + south))
-            new = 0.5 * half if p == 0 else half - basis[p - 1, here]
+            half = a4[here] * k0 - half_wet(r) * (vert + side)
+            new = 0.5 * half if p == 0 else half - field(p - 1, r)
             basis[p + 1, here] = new
+            held[p + 1, r] = new
             if summed[0] <= r < summed[1]:
                 kept = in_window(r, k0)
                 squares.append(kept * kept)
                 crosses.append(kept * in_window(r, new))
-                if p + 1 == SWEEPS:
-                    lasts.append(in_window(r, new) * in_window(r, new))
-        return [tree([fold(t) for t in x]) for x in (squares, crosses, lasts) if x]
+        for key in [key for key in held if key[0] < p]:
+            del held[key]
+        return [tree([fold(t) for t in x]) for x in (squares, crosses) if x]
 
     def floor8(x):
         return x // 8 * 8
@@ -392,7 +429,7 @@
     for p in range(SWEEPS):
         j = p + 1
         sums = sweep(
-            p, floor8(2 + j), ceil8(rows - 2 - j), 0, rows, lambda r: own, (inner_from, inner_to)
+            p, floor8(2 + j), ceil8(rows - 2 - j), 0, rows, lambda r: half_own, (inner_from, inner_to)
         )
         for i, x in enumerate(sums):
             acc[2 * p + i] = x
@@ -451,11 +488,13 @@
         basis[0, pl.ds(WEST + rows, 8)] = f_high
         for r in range(8, EAST, 8):
             basis[0, pl.ds(WEST + rows + r, 8)] = fe_rx[pl.ds(r, 8)]
+        held = {}
+        half_east = 0.5 * east
         for p in range(SWEEPS):
             j = p + 1
             sweep(
                 p, floor8(rows - 2 - j), ceil8(rows + SWEEPS - j), 0, rows + EAST,
-                lambda r: own if r < rows else east, (0, 0),
+                lambda r: half_own if r < rows else half_east, (0, 0), held,
             )
 
     def before_west():
@@ -479,19 +518,20 @@
     basis[0, pl.ds(WEST, 8)] = f_high
 
     moments = [None] * MOMENTS
-    base = [None, None]
+    west_held = {}
+    half_west = 0.5 * west
     for p in range(SWEEPS):
         j = p + 1
         sums = sweep(
             p, floor8(j - 2 * SWEEPS - 2), ceil8(2 + j) if j < SWEEPS else inner_from, -WEST, rows,
-            lambda r: west if r < 0 else own, (floor8(-SHIFT), 8),
+            lambda r: half_west if r < 0 else half_own, (floor8(-SHIFT), 8), west_held,
         )
         for i, x in enumerate(sums):
             moments[2 * p + i] = x
         tail = []
         for r in range(8, inner_from, 8):
             k0, k1 = basis[p, pl.ds(WEST + r, 8)], basis[p + 1, pl.ds(WEST + r, 8)]
-            tail.append((k0 * k0, k0 * k1) + ((k1 * k1,) if j == SWEEPS else ()))
+            tail.append((k0 * k0, k0 * k1))
         for i in range(len(sums)):
             moments[2 * p + i] = tree(
                 [moments[2 * p + i], acc[2 * p + i]] + [fold(t[i]) for t in tail]
@@ -557,13 +597,12 @@
         store.start()
     row = mom[...]
     m = [jnp.broadcast_to(row[:, i : i + 1], (8, 128)) for i in range(MOMENTS)]
-    gram = [[m[a + b] + m[abs(a - b)] for b in range(FIELDS)] for a in range(FIELDS)]
-    offset, resid = inner_steps(gram, SWEEPS)
+    offset, resid = inner_steps(m, SWEEPS)
 
     def combine(vals, coef):
         return tree([c * v for v, c in zip(vals, coef) if c is not None])
 
-    parts = 2
+    parts = 4
     step = rows // 8 // parts
     for part in range(parts):
         for s in range(part * step, (part + 1) * step):

time: 16.5 us -> 16.1 us (0.976)
  Pallas kernels: 15.7 us -> 15.3 us
    pallas_call x1, Pallas kernels: 13.9 us -> 13.7 us  [on_device(): pl.pallas_call(functools.partial(kernel, n), out_shape=mids, in_specs=[hb...]
where the time goes in v3:
time: 16.1 us; the launch traced here: 16 us
  Pallas kernels  15.3 us (95%)
  between operations  0.64 us (4%)
    pallas_call x1, Pallas kernels, on_device(): pl.pallas_call(functools.partial(kernel, n), out_shape=mids, in_specs=[hb...  13.7 us
    pallas_call x1, Pallas kernels, on_device(): pl.pallas_call(finish, out_shape=tuple((pltpu.HBM(x.shape, x.dtype) for x...  1.68 us

profile of v3, /device:TPU:0, one launch (start us, length us, event | category | flops | bytes accessed | tf_op | source)
XLA Modules:
  0.0 16.0 jit_solution(8775904683201979286)
XLA Ops:
  0.6 13.7 %shard_map.118 = (bf16[4,96,512]{2,1,0:T(8,128)(2,1)S(1)}, bf16[4,96,512]{2,1,0:T(8,128)(2,1)S(1)}, bf16[4,96,512]{2,1,0:T(8,128)(2,1)S(1)}, bf16[4,96,512]{2,1,...) custom-call(f32[4,96,512]{2,1,0:T(8,128)} %heat.1, f32[4,96,512]{2,1,0:T(8,128)} %salt.1, ...), custom_call_target="tpu_custom_call" | custom-call | tf_op jit(solution)/shard_map/pallas_call | solution.py:643
  14.3 1.7 %shard_map.119 = (bf16[4,96,512]{2,1,0:T(8,128)(2,1)}, bf16[4,96,512]{2,1,0:T(8,128)(2,1)}, bf16[4,96,512]{2,1,0:T(8,128)(2,1)}, bf16[4,96,512]{2,1,0:T(8,128)(2...) custom-call(bf16[4,96,512]{2,1,0:T(8,128)(2,1)S(1)} %get-tuple-element.12.bh, bf16[4,96,512]{2,1,0:T(8,128)(2,1)S(1)} %get-tuple-element.13.bs, ...), custom_call_target="tpu_custom_call" | custom-call | tf_op jit(solution)/shard_map/pallas_call | solution.py:683

commit v4 on v3

--- a/solution.py
+++ b/solution.py
@@ -42,16 +42,6 @@
     return terms[0]
 
 
-def square(even, coef):
-    rows = []
-    for i, ci in enumerate(coef):
-        if ci is not None:
-            row = [(even[2 * i] + even[0]) * ci]
-            row += [2.0 * (even[i + j] + even[i - j]) * coef[j] for j in range(i)]
-            rows.append(ci * tree(row))
-    return tree(rows)
-
-
 def plus(a, b):
     if a is None:
         return b
@@ -64,39 +54,53 @@
     return None if a is None else scale * a
 
 
-def inner_steps(moments, sweeps):
+def inner_steps(m, sweeps):
     extent = sweeps + 1
     table = shift_table(extent)
-    one = jnp.ones_like(moments[0])
-    along = [one] + [None] * sweeps
-    resid = [one] + [None] * sweeps
-    offset = [None] * extent
-    norm_now = moments[0] + moments[0]
-    for sweep in range(sweeps):
-        image = []
+    ones = jnp.ones_like(m[0])
+    pushed = [0.25 * (m[k + 1] + m[abs(k - 1)]) + 0.5 * m[k] for k in range(2 * sweeps - 1)]
+    a = [[pushed[i + j] + pushed[i - j] for j in range(i + 1)] for i in range(sweeps)]
+    lower = [[None] * sweeps for _ in range(sweeps)]
+    inverse = []
+    y = [m[i] + m[i] for i in range(sweeps)]
+    for k in range(sweeps):
+        inverse.append(ones / a[k][k])
+        for i in range(k + 1, sweeps):
+            lower[i][k] = a[i][k] * inverse[k]
+        for i in range(k + 1, sweeps):
+            for j in range(k + 1, i + 1):
+                a[i][j] = a[i][j] - lower[i][k] * a[j][k]
+            y[i] = y[i] - lower[i][k] * y[k]
+
+    def backward(y):
+        z = [v * d for v, d in zip(y, inverse)]
+        for i in range(sweeps - 1, 0, -1):
+            for j in range(i):
+                z[j] = z[j] - lower[i][j] * z[i]
+        return z
+
+    def image(c):
+        out = []
         for i in range(extent):
             total = None
-            for j in range(extent):
+            for j in range(sweeps):
                 if table[i, j] != 0.0:
-                    total = plus(total, scaled(float(table[i, j]), along[j]))
-            image.append(total)
-        scale = 1.0 / norm_now
-        rows = []
-        for i, ai in enumerate(along):
-            if ai is not None:
-                row = [
-                    (moments[i + j] + moments[abs(i - j)]) * image[j]
-                    for j in range(extent) if image[j] is not None
-                ]
-                rows.append(ai * tree(row))
-        alpha = norm_now / tree(rows)
-        offset = [plus(o, scaled(alpha, a)) for o, a in zip(offset, along)]
-        resid = [plus(r, scaled(-alpha, a)) for r, a in zip(resid, image)]
-        if sweep + 1 < sweeps:
-            norm_next = square(moments, resid)
-            beta = norm_next * scale
-            along = [plus(r, scaled(beta, a)) for r, a in zip(resid, along)]
-            norm_now = norm_next
+                    total = plus(total, scaled(float(table[i, j]), c[j]))
+            out.append(total)
+        return out
+
+    offset = backward(y)
+    resid = [-x for x in image(offset)]
+    resid[0] = resid[0] + ones
+    y = [
+        tree([(m[i + j] + m[abs(i - j)]) * resid[j] for j in range(extent)]) for i in range(sweeps)
+    ]
+    for i in range(sweeps):
+        for j in range(i + 1, sweeps):
+            y[j] = y[j] - lower[j][i] * y[i]
+    more = backward(y)
+    offset = [c + d for c, d in zip(offset, more)]
+    resid = [r - x for r, x in zip(resid, image(more))]
     return offset, resid
 
 
@@ -105,7 +109,7 @@
     heat, salt, uvel, vvel, spacing, damp, flags,
     bh, bs, bu, bv, basis, mom,
     ue, ve, he, se, ef, nf, ff, de, tu, tv, acc, edges,
-    uv_tx, hs_tx, uv_rx, hs_rx, aw_tx, ae_tx, a4, fw_tx, fe_tx, fw_rx, fe_rx, slots,
+    uv_tx, hs_tx, uv_rx, hs_rx, mix_tx, mix_rx, fx_tx, fx_rx, ae_tx, a4, fw_tx, fe_tx, fw_rx, fe_rx, slots,
     space, marks,
     flux_e, lsem, ssem, rsem, gsem, late_sem,
 ):
@@ -113,6 +117,7 @@
     me = lax.axis_index("blk")
     right, left = lax.rem(me + 1, n), lax.rem(me + n - 1, n)
     late = rows - WEST
+    west_rows = 2 * (WEST - 8) + (mix_tx.shape[0] + fx_tx.shape[0]) * 128 // lanes
     split = late - 8
 
     def part(ref, buf, lo, hi, sem):
@@ -127,11 +132,12 @@
     loads = [
         pltpu.make_async_copy(flags, marks, lsem.at[0]),
         pltpu.make_async_copy(spacing, space, lsem.at[1]),
-        pltpu.make_async_copy(damp, de, lsem.at[3]),
+        pltpu.make_async_copy(damp.at[pl.ds(late, WEST)], de.at[pl.ds(late, WEST)], lsem.at[3]),
         part(uvel, ue, split, rows, 2),
         part(vvel, ve, split, rows, 2),
         part(uvel, ue, 0, split, 4),
         part(vvel, ve, 0, split, 4),
+        pltpu.make_async_copy(damp.at[pl.ds(0, late)], de.at[pl.ds(0, late)], lsem.at[6]),
     ]
     more = [
         pltpu.make_async_copy(heat, he, lsem.at[5]),
@@ -326,23 +332,43 @@
         ).wait_recv()
 
     def send_left():
-        send(uv_tx.at[0], uv_rx.at[1], 1, left)
+        send(uv_tx.at[0], uv_rx, 1, left)
         send(ae_tx, a4.at[pl.ds(WEST + rows, EAST)], 1, left)
         send(fe_tx, fe_rx, 1, left)
 
+    chunks = lanes // 128
+
+    def pack(ref, base, items):
+        packed = {}
+        for i, (x, place) in enumerate(items):
+            for c in range(chunks):
+                group, spot = divmod(i * chunks + c, 8)
+                t = x[:, 128 * c : 128 * c + 128]
+                if (spot - place) % 8:
+                    t = pltpu.roll(t, (spot - place) % 8, 0)
+                packed[group] = jnp.where(sub[:, :128] == spot, t, packed[group]) if group in packed else t
+        for group, x in packed.items():
+            ref[pl.ds(base + 8 * group, 8)] = x
+
+    def unpack(ref, base, i):
+        return jnp.concatenate(
+            [jnp.broadcast_to(ref[pl.ds(base + i * chunks + c, 1)], (8, 128)) for c in range(chunks)], axis=1
+        )
+
+    def damping(first, last):
+        for r in range(first, last, 8):
+            a4[pl.ds(WEST + r, 8)] = 0.5 * (own * (6.0 + de[pl.ds(r, 8)]) + (1.0 - own)) - 2.0
+
     loads[2].wait()
-    for r in range(0, rows, 8):
-        a = 0.5 * (own * (6.0 + de[pl.ds(r, 8)]) + (1.0 - own)) - 2.0
-        a4[pl.ds(WEST + r, 8)] = a
-        if r >= late:
-            aw_tx[pl.ds(r - late, 8)] = jnp.where(top, own, a) if r == late else a
-        if r < EAST:
-            ae_tx[pl.ds(r, 8)] = jnp.where(bottom, own, a) if r + 8 == EAST else a
+    damping(late, rows)
+    pack(mix_tx, 8 * chunks, [(a4[pl.ds(WEST + late, 8)], 7), (own, 7)])
     pair(split, rows, 2).wait()
     uv_tx[1] = gather_row((ue, ve), rows - 1)
+    for c in range(chunks):
+        mix_tx[pl.ds(8 * c, 8)] = uv_tx[1, :, 128 * c : 128 * c + 128]
     pass_barrier()
-    send(uv_tx.at[1], uv_rx.at[0], 0, right)
-    send(aw_tx, a4.at[pl.ds(0, WEST)], 0, right)
+    send(mix_tx, mix_rx, 0, right)
+    send(a4.at[pl.ds(WEST + late + 8, WEST - 8)], a4.at[pl.ds(8, WEST - 8)], 0, right)
     tell_earlier()
     for load in more:
         load.start()
@@ -352,13 +378,19 @@
         f = forcing(r, late, rows)
         if r > late:
             basis[0, pl.ds(WEST + r, 8)] = f
+            fw_tx[pl.ds(r - late - 8, 8)] = f
         else:
-            f = jnp.where(top, jnp.broadcast_to(tu[pl.ds(rows - 1, 1)], (8, lanes)), f)
-        fw_tx[pl.ds(r - late, 8)] = f
+            pack(fx_tx, 0, [(f, 6), (f, 7), (tu[pl.ds(rows - 8, 8)], 7)])
     send(fw_tx, fw_rx, 0, right)
+    send(fx_tx, fx_rx, 0, right)
 
     pair(0, split, 4).wait()
     uv_tx[0] = gather_row((ue, ve), 0)
+    loads[7].wait()
+    damping(0, late)
+    for r in range(0, EAST, 8):
+        a = a4[pl.ds(WEST + r, 8)]
+        ae_tx[pl.ds(r, 8)] = jnp.where(bottom, own, a) if r + 8 == EAST else a
     north_flux(0, late, (ue, ve), True)
     flows(0, late, (ue, ve), (bu, bv), 0, True)
     for r in range(0, late + 8, 8):
@@ -480,7 +512,7 @@
         arrive(1, 2 * EAST + 8)
         east = row_of(a4, WEST + rows + EAST - 1)
         _, flux, f_low, f_high = seam(
-            uv_tx[1], uv_rx[1], own, east, row_of(tu, rows - 1), row_of(fe_rx, EAST - 1),
+            uv_tx[1], uv_rx[...], own, east, row_of(tu, rows - 1), row_of(fe_rx, EAST - 1),
             basis[0, pl.ds(WEST + rows - 8, 8)], fe_rx[pl.ds(0, 8)],
         )
         flux_e[...] = flux
@@ -506,14 +538,17 @@
 
     pl.when(at_start)(before_west)
 
-    arrive(0, 2 * WEST + 8)
-    west = row_of(a4, 0)
+    arrive(0, west_rows)
+    west = unpack(mix_rx, 8 * chunks, 1)
+    a4[pl.ds(0, 8)] = unpack(mix_rx, 8 * chunks, 0)
+    uv_west = jnp.concatenate([mix_rx[pl.ds(8 * c, 8)] for c in range(chunks)], axis=1)
     speed_w, flux_w, f_low, f_high = seam(
-        uv_rx[0], uv_tx[0], west, own, row_of(fw_rx, 0), row_of(tu, 0),
-        fw_rx[pl.ds(WEST - 8, 8)], basis[0, pl.ds(WEST, 8)],
+        uv_west, uv_tx[0], west, own, unpack(fx_rx, 0, 2), row_of(tu, 0),
+        fw_rx[pl.ds(WEST - 16, 8)], basis[0, pl.ds(WEST, 8)],
     )
-    for r in range(0, WEST - 8, 8):
-        basis[0, pl.ds(r, 8)] = fw_rx[pl.ds(r, 8)]
+    basis[0, pl.ds(0, 8)] = jnp.where(bottom, unpack(fx_rx, 0, 1), unpack(fx_rx, 0, 0))
+    for r in range(8, WEST - 8, 8):
+        basis[0, pl.ds(r, 8)] = fw_rx[pl.ds(r - 8, 8)]
     basis[0, pl.ds(WEST - 8, 8)] = f_low
     basis[0, pl.ds(WEST, 8)] = f_high
 
@@ -568,7 +603,7 @@
     mend((bu, bv), edges[0] + (COURANT * own) * flux_w, 0)
     mend((bu, bv), edges[1] - (COURANT * own) * flux_e[...], rows - 1)
     east = row_of(a4, WEST + rows + EAST - 1)
-    speed_e = face(uv_tx[1], uv_rx[1], own * east)
+    speed_e = face(uv_tx[1], uv_rx[...], own * east)
     mend((bh, bs), edges[2] + (COURANT * own) * carried(speed_w, hs_rx[0], hs_tx[0]), 0)
     mend((bh, bs), edges[3] - (COURANT * own) * carried(speed_e, hs_tx[1], hs_rx[1]), rows - 1)
 
@@ -580,7 +615,7 @@
     rest.wait_recv()
     mom[...] = jnp.broadcast_to(tree([slots[i] for i in range(n)]), (8, 128))
     rest.wait_send()
-    lot = a4.at[pl.ds(0, 2 * WEST + 2 * EAST + 32)]
+    lot = a4.at[pl.ds(0, west_rows + 2 * EAST + 24)]
     pltpu.make_async_remote_copy(
         src_ref=lot, dst_ref=lot, send_sem=ssem.at[0], recv_sem=rsem.at[0],
         device_id={"blk": right}, device_id_type=pl.DeviceIdType.MESH,
@@ -602,7 +637,7 @@
     def combine(vals, coef):
         return tree([c * v for v, c in zip(vals, coef) if c is not None])
 
-    parts = 4
+    parts = 2
     step = rows // 8 // parts
     for part in range(parts):
         for s in range(part * step, (part + 1) * step):
@@ -624,6 +659,9 @@
     n = lax.axis_size("blk")
     levels, rows, lanes = uvel.shape
     total = WEST + rows + EAST
+    chunks = lanes // 128
+    mixed, extra = 8 * chunks + -(-2 * chunks // 8) * 8, -(-3 * chunks // 8) * 8
+    extra += -(mixed + extra) % (8 * chunks)
     hbm = pl.BlockSpec(memory_space=pltpu.HBM)
     vmem = pl.BlockSpec(memory_space=pltpu.VMEM)
     args = [
@@ -655,20 +693,23 @@
             vm((4, 8, lanes), F32),
             vm((2, 8, lanes), F32),
             vm((2, 8, lanes), F32),
+            vm((8, lanes), F32),
             vm((2, 8, lanes), F32),
-            vm((2, 8, lanes), F32),
-            vm((WEST, lanes), F32),
+            vm((mixed, 128), F32),
+            vm((mixed, 128), F32),
+            vm((extra, 128), F32),
+            vm((extra, 128), F32),
             vm((EAST, lanes), F32),
             vm((total, lanes), F32),
-            vm((WEST, lanes), F32),
+            vm((WEST - 8, lanes), F32),
             vm((EAST, lanes), F32),
-            vm((WEST, lanes), F32),
+            vm((WEST - 8, lanes), F32),
             vm((EAST, lanes), F32),
             vm((n, 1, 128), F32),
             pltpu.SMEM(spacing.shape, F32),
             pltpu.SMEM(flags.shape, flags.dtype),
             vm((8, lanes), F32),
-            dma((6,)),
+            dma((7,)),
             dma((1,)),
             dma((3,)),
             dma((2,)),

time: 16.1 us -> 15.7 us (0.975)
  Pallas kernels: 15.3 us -> 14.9 us
    pallas_call x1, Pallas kernels: 1.68 us -> 1.31 us  [on_device(): pl.pallas_call(finish, out_shape=tuple((pltpu.HBM(x.shape, x.dtype) for x...]
where the time goes in v4:
time: 15.7 us; the launch traced here: 15.5 us
  Pallas kernels  14.9 us (95%)
  between operations  0.64 us (4%)
    pallas_call x1, Pallas kernels, on_device(): pl.pallas_call(functools.partial(kernel, n), out_shape=mids, in_specs=[hb...  13.5 us
    pallas_call x1, Pallas kernels, on_device(): pl.pallas_call(finish, out_shape=tuple((pltpu.HBM(x.shape, x.dtype) for x...  1.31 us

profile of v4, /device:TPU:0, one launch (start us, length us, event | category | flops | bytes accessed | tf_op | source)
XLA Modules:
  0.0 15.5 jit_solution(13600110484721437264)
XLA Ops:
  0.6 13.5 %shard_map.118 = (bf16[4,96,512]{2,1,0:T(8,128)(2,1)S(1)}, bf16[4,96,512]{2,1,0:T(8,128)(2,1)S(1)}, bf16[4,96,512]{2,1,0:T(8,128)(2,1)S(1)}, bf16[4,96,512]{2,1,...) custom-call(f32[4,96,512]{2,1,0:T(8,128)} %heat.1, f32[4,96,512]{2,1,0:T(8,128)} %salt.1, ...), custom_call_target="tpu_custom_call" | custom-call | tf_op jit(solution)/shard_map/pallas_call | solution.py:681
  14.2 1.3 %shard_map.119 = (bf16[4,96,512]{2,1,0:T(8,128)(2,1)}, bf16[4,96,512]{2,1,0:T(8,128)(2,1)}, bf16[4,96,512]{2,1,0:T(8,128)(2,1)}, bf16[4,96,512]{2,1,0:T(8,128)(2...) custom-call(bf16[4,96,512]{2,1,0:T(8,128)(2,1)S(1)} %get-tuple-element.12.bh, bf16[4,96,512]{2,1,0:T(8,128)(2,1)S(1)} %get-tuple-element.13.bs, ...), custom_call_target="tpu_custom_call" | custom-call | tf_op jit(solution)/shard_map/pallas_call | solution.py:724

commit v5 on v4

--- a/solution.py
+++ b/solution.py
@@ -137,15 +137,12 @@
         part(vvel, ve, split, rows, 2),
         part(uvel, ue, 0, split, 4),
         part(vvel, ve, 0, split, 4),
-        pltpu.make_async_copy(damp.at[pl.ds(0, late)], de.at[pl.ds(0, late)], lsem.at[6]),
+        pltpu.make_async_copy(damp.at[pl.ds(0, late)], de.at[pl.ds(0, late)], lsem.at[5]),
     ]
     more = [
-        pltpu.make_async_copy(heat, he, lsem.at[5]),
-        pltpu.make_async_copy(salt, se, lsem.at[5]),
+        pltpu.make_async_copy(heat, he, lsem.at[2]),
+        pltpu.make_async_copy(salt, se, lsem.at[2]),
     ]
-    for load in loads[:5]:
-        load.start()
-
     barrier = pltpu.get_barrier_semaphore()
 
     def tell(sem, to):
@@ -155,6 +152,8 @@
 
     at_start, at_end = me == 0, me == n - 1
     pl.when(me > 0)(lambda: tell(barrier, left))
+    for load in loads[:5]:
+        load.start()
     for k in range(1, n):
         pl.when(me + k < n)(functools.partial(tell, barrier, lax.rem(me + k, n)))
     for load in loads[5:]:
@@ -466,7 +465,7 @@
         for i, x in enumerate(sums):
             acc[2 * p + i] = x
 
-    pltpu.make_async_copy(ff, ff, lsem.at[5]).wait()
+    pltpu.make_async_copy(ff, ff, lsem.at[2]).wait()
     hs_tx[0] = gather_row((he, se), 0)
     hs_tx[1] = gather_row((he, se), rows - 1)
     send(hs_tx.at[1], hs_rx.at[0], 2, right)
@@ -709,7 +708,7 @@
             pltpu.SMEM(spacing.shape, F32),
             pltpu.SMEM(flags.shape, flags.dtype),
             vm((8, lanes), F32),
-            dma((7,)),
+            dma((6,)),
             dma((1,)),
             dma((3,)),
             dma((2,)),

time: 15.7 us -> 15.7 us (level)
  no operation moved by 1% of the time
where the time goes in v5:
time: 15.7 us; the launch traced here: 15.5 us
  Pallas kernels  14.9 us (95%)
  between operations  0.64 us (4%)
    pallas_call x1, Pallas kernels, on_device(): pl.pallas_call(functools.partial(kernel, n), out_shape=mids, in_specs=[hb...  13.6 us
    pallas_call x1, Pallas kernels, on_device(): pl.pallas_call(finish, out_shape=tuple((pltpu.HBM(x.shape, x.dtype) for x...  1.31 us

profile of v5, /device:TPU:0, one launch (start us, length us, event | category | flops | bytes accessed | tf_op | source)
XLA Modules:
  0.0 15.5 jit_solution(17361416604103401203)
XLA Ops:
  0.6 13.6 %shard_map.118 = (bf16[4,96,512]{2,1,0:T(8,128)(2,1)S(1)}, bf16[4,96,512]{2,1,0:T(8,128)(2,1)S(1)}, bf16[4,96,512]{2,1,0:T(8,128)(2,1)S(1)}, bf16[4,96,512]{2,1,...) custom-call(f32[4,96,512]{2,1,0:T(8,128)} %heat.1, f32[4,96,512]{2,1,0:T(8,128)} %salt.1, ...), custom_call_target="tpu_custom_call" | custom-call | tf_op jit(solution)/shard_map/pallas_call | solution.py:680
  14.2 1.3 %shard_map.119 = (bf16[4,96,512]{2,1,0:T(8,128)(2,1)}, bf16[4,96,512]{2,1,0:T(8,128)(2,1)}, bf16[4,96,512]{2,1,0:T(8,128)(2,1)}, bf16[4,96,512]{2,1,0:T(8,128)(2...) custom-call(bf16[4,96,512]{2,1,0:T(8,128)(2,1)S(1)} %get-tuple-element.12.bh, bf16[4,96,512]{2,1,0:T(8,128)(2,1)S(1)} %get-tuple-element.13.bs, ...), custom_call_target="tpu_custom_call" | custom-call | tf_op jit(solution)/shard_map/pallas_call | solution.py:723

commit v6 on v5

--- a/solution.py
+++ b/solution.py
@@ -117,7 +117,8 @@
     me = lax.axis_index("blk")
     right, left = lax.rem(me + 1, n), lax.rem(me + n - 1, n)
     late = rows - WEST
-    west_rows = 2 * (WEST - 8) + (mix_tx.shape[0] + fx_tx.shape[0]) * 128 // lanes
+    chunks = lanes // 128
+    west_rows = 2 * (WEST - 8) * chunks + mix_tx.shape[0] + fx_tx.shape[0]
     split = late - 8
 
     def part(ref, buf, lo, hi, sem):
@@ -323,8 +324,11 @@
             device_id={"blk": to}, device_id_type=pl.DeviceIdType.MESH,
         ).start()
 
-    def arrive(sem, height):
-        lot = a4.at[pl.ds(0, height)]
+    def lot_of(count):
+        return acc.at[pl.ds(0, count // 8)]
+
+    def arrive(sem, count):
+        lot = lot_of(count)
         pltpu.make_async_remote_copy(
             src_ref=lot, dst_ref=lot, send_sem=ssem.at[0], recv_sem=rsem.at[sem],
             device_id={"blk": right}, device_id_type=pl.DeviceIdType.MESH,
@@ -334,8 +338,6 @@
         send(uv_tx.at[0], uv_rx, 1, left)
         send(ae_tx, a4.at[pl.ds(WEST + rows, EAST)], 1, left)
         send(fe_tx, fe_rx, 1, left)
-
-    chunks = lanes // 128
 
     def pack(ref, base, items):
         packed = {}
@@ -365,10 +367,14 @@
     uv_tx[1] = gather_row((ue, ve), rows - 1)
     for c in range(chunks):
         mix_tx[pl.ds(8 * c, 8)] = uv_tx[1, :, 128 * c : 128 * c + 128]
-    pass_barrier()
-    send(mix_tx, mix_rx, 0, right)
-    send(a4.at[pl.ds(WEST + late + 8, WEST - 8)], a4.at[pl.ds(8, WEST - 8)], 0, right)
-    tell_earlier()
+    def open_right():
+        pass_barrier()
+        send(mix_tx, mix_rx, 0, right)
+        send(a4.at[pl.ds(WEST + late + 8, WEST - 8)], a4.at[pl.ds(8, WEST - 8)], 0, right)
+        tell_earlier()
+
+    waits = (lax.rem(me, 2) == 1) & (me < n - 1)
+    pl.when(jnp.logical_not(waits))(open_right)
     for load in more:
         load.start()
     north_flux(late, rows, (ue, ve), True)
@@ -380,6 +386,7 @@
             fw_tx[pl.ds(r - late - 8, 8)] = f
         else:
             pack(fx_tx, 0, [(f, 6), (f, 7), (tu[pl.ds(rows - 8, 8)], 7)])
+    pl.when(waits)(open_right)
     send(fw_tx, fw_rx, 0, right)
     send(fx_tx, fx_rx, 0, right)
 
@@ -508,7 +515,7 @@
     def tracers_and_east(both=True):
         if both:
             tracers()
-        arrive(1, 2 * EAST + 8)
+        arrive(1, (2 * EAST + 8) * chunks)
         east = row_of(a4, WEST + rows + EAST - 1)
         _, flux, f_low, f_high = seam(
             uv_tx[1], uv_rx[...], own, east, row_of(tu, rows - 1), row_of(fe_rx, EAST - 1),
@@ -585,7 +592,7 @@
         ).start()
 
     pl.when(me > 0)(tracers_and_east)
-    arrive(2, 16)
+    arrive(2, 16 * chunks)
 
     def mend(outs, fixed, row):
         block, place = row // 8 * 8, row % 8
@@ -614,7 +621,7 @@
     rest.wait_recv()
     mom[...] = jnp.broadcast_to(tree([slots[i] for i in range(n)]), (8, 128))
     rest.wait_send()
-    lot = a4.at[pl.ds(0, west_rows + 2 * EAST + 24)]
+    lot = lot_of(west_rows + (2 * EAST + 24) * chunks)
     pltpu.make_async_remote_copy(
         src_ref=lot, dst_ref=lot, send_sem=ssem.at[0], recv_sem=rsem.at[0],
         device_id={"blk": right}, device_id_type=pl.DeviceIdType.MESH,
@@ -660,7 +667,6 @@
     total = WEST + rows + EAST
     chunks = lanes // 128
     mixed, extra = 8 * chunks + -(-2 * chunks // 8) * 8, -(-3 * chunks // 8) * 8
-    extra += -(mixed + extra) % (8 * chunks)
     hbm = pl.BlockSpec(memory_space=pltpu.HBM)
     vmem = pl.BlockSpec(memory_space=pltpu.VMEM)
     args = [
@@ -688,7 +694,7 @@
             vm((rows, lanes), F32),
             vm((rows, lanes), F32),
             vm((rows, lanes), F32),
-            vm((MOMENTS, 8, 128), F32),
+            vm((max(MOMENTS, (total + WEST) * chunks // 8), 8, 128), F32),
             vm((4, 8, lanes), F32),
             vm((2, 8, lanes), F32),
             vm((2, 8, lanes), F32),

time: 15.7 us -> 15.6 us (level)
  no operation moved by 1% of the time
where the time goes in v6:
time: 15.6 us; the launch traced here: 15.5 us
  Pallas kernels  14.8 us (95%)
  between operations  0.64 us (4%)
    pallas_call x1, Pallas kernels, on_device(): pl.pallas_call(functools.partial(kernel, n), out_shape=mids, in_specs=[hb...  13.5 us
    pallas_call x1, Pallas kernels, on_device(): pl.pallas_call(finish, out_shape=tuple((pltpu.HBM(x.shape, x.dtype) for x...  1.31 us

profile of v6, /device:TPU:0, one launch (start us, length us, event | category | flops | bytes accessed | tf_op | source)
XLA Modules:
  0.0 15.5 jit_solution(9650288931754816227)
XLA Ops:
  0.6 13.5 %shard_map.118 = (bf16[4,96,512]{2,1,0:T(8,128)(2,1)S(1)}, bf16[4,96,512]{2,1,0:T(8,128)(2,1)S(1)}, bf16[4,96,512]{2,1,0:T(8,128)(2,1)S(1)}, bf16[4,96,512]{2,1,...) custom-call(f32[4,96,512]{2,1,0:T(8,128)} %heat.1, f32[4,96,512]{2,1,0:T(8,128)} %salt.1, ...), custom_call_target="tpu_custom_call" | custom-call | tf_op jit(solution)/shard_map/pallas_call | solution.py:686
  14.2 1.3 %shard_map.119 = (bf16[4,96,512]{2,1,0:T(8,128)(2,1)}, bf16[4,96,512]{2,1,0:T(8,128)(2,1)}, bf16[4,96,512]{2,1,0:T(8,128)(2,1)}, bf16[4,96,512]{2,1,0:T(8,128)(2...) custom-call(bf16[4,96,512]{2,1,0:T(8,128)(2,1)S(1)} %get-tuple-element.12.bh, bf16[4,96,512]{2,1,0:T(8,128)(2,1)S(1)} %get-tuple-element.13.bs, ...), custom_call_target="tpu_custom_call" | custom-call | tf_op jit(solution)/shard_map/pallas_call | solution.py:729
